TPU v7x, 256 devices: a whole 4x4x8 slice. The times are simulated.
256 devices in a mesh: space: 8 (over y_hi, x), vel: 32 (over z, y_lo, core).
Axes of the slice: x: 4, y: 4 (y_hi: 2, y_lo: 2; y = y_hi * 2 + y_lo), z: 8, core: 2. Of those that a mesh axis runs over, the one named last changes fastest.
Arguments:
- distribution: float32 [8, 16, 16, 32768], P('space', None, None, 'vel'), may hold values from 0.003 to 450, as said below
- inflow: float32 [2, 16, 16, 32768], P(None, None, None, 'vel'), may hold values from 0.3 to 3
- wall_temp: float32 [2, 16, 16], replicated, may hold values from 0.5 to 4
- face_type: int32 [2, 16, 16], replicated, may hold values from 0 to 2
Outputs:
- updated: float32 [8, 16, 16, 32768], P('space', None, None, 'vel')
- fields: float32 [8, 8, 16, 16], P(None, 'space')
Inputs may be any that keep to these rules, and one draw needn't show every extreme that they name: `distribution`: every entry is positive.
All inputs are finite; a program needn't handle non-finite values.
Results may differ from a plain program's by a relative error of at most 0.0003.
Values sent between devices are 32-bit elements; how exact they have to be, the bound alone decides.
No kernel may reach another device: no remote copies, remote signals or barrier semaphores. Data moves between devices by JAX's collectives and lax.ppermute only.
A program may use at most 64 MiB of HBM per device.

v0:
```python
import jax
import jax.numpy as jnp
import numpy as np
from jax import lax
from jax.experimental import pallas as pl
from jax.experimental.pallas import tpu as pltpu
from jax.sharding import Mesh, PartitionSpec as P


NV = 32768
CELLS = 256
HALF = 512
NK = 13
ROWS = 112
HROWS = ROWS // 2
courant = 0.08
rate_field = 0.8
box_volume = 512.0
HIGHEST = lax.Precision.HIGHEST
f32 = jnp.float32

MOMENTS = [
    [(0, 0, 0)],
    [(1, 0, 0)],
    [(0, 1, 0)],
    [(0, 0, 1)],
    [(2, 0, 0)],
    [(0, 2, 0)],
    [(0, 0, 2)],
    [(1, 1, 0)],
    [(1, 0, 1)],
    [(0, 1, 1)],
    [(3, 0, 0), (1, 2, 0), (1, 0, 2)],
    [(2, 1, 0), (0, 3, 0), (0, 1, 2)],
    [(2, 0, 1), (0, 2, 1), (0, 0, 3)],
]


def axis_tables():
    grid = (np.arange(32) + 0.5) * 0.25 - 4.0
    plus, minus = courant * np.maximum(grid, 0.0), courant * np.maximum(-grid, 0.0)
    table = np.zeros((96, 96))
    for axis in range(3):
        for power in range(4):
            for d in range(7):
                row = grid**power
                if d == 1 + 2 * axis:
                    row = row * plus
                if d == 2 + 2 * axis:
                    row = row * minus
                table[32 * axis + 8 * power + d, 32 * axis : 32 * axis + 32] = row
    walls = []
    for weight in (plus, minus):
        wall = table.copy()
        wall[:32, :32] *= weight
        walls.append(np.concatenate([table, wall]))
    return table.astype(np.float32), np.stack(walls).astype(np.float32)


TABLE, WALL_TABLES = axis_tables()


def dot(a, b):
    return lax.dot_general(a, b, (((1,), (0,)), ((), ())), precision=HIGHEST, preferred_element_type=f32)


def dot_t(a, b):
    return lax.dot_general(a, b, (((1,), (1,)), ((), ())), precision=HIGHEST, preferred_element_type=f32)


def tile4(a):
    return jnp.concatenate([a] * 4, 0)


def speed_grid():
    return (lax.broadcasted_iota(jnp.int32, (32, CELLS), 0).astype(f32) + 0.5) * 0.25 - 4.0


def lane_speeds(p, rows):
    lane = lax.broadcasted_iota(jnp.int32, (rows, HALF), 1)
    cy = ((lane // 32 + (p % 2) * 16).astype(f32) + 0.5) * 0.25 - 4.0
    cz = ((lane % 32).astype(f32) + 0.5) * 0.25 - 4.0
    return cy, cz


def speed_x(p):
    return ((p // 2).astype(f32) + 0.5) * 0.25


def to_columns(rows):
    pad = 128 - rows.shape[0]
    return jnp.transpose(jnp.concatenate([rows, jnp.zeros((pad, CELLS), f32)], 0))


def equilibrium_moments(params, table):
    n, ux, uy, uz, temp, qx, qy, qz = params
    inv = 1.0 / temp
    two_pi = 2.0 * np.pi * temp
    pref = n * box_volume / (two_pi * jnp.sqrt(two_pi))
    scale = inv * inv / (15.0 * n)
    grid = speed_grid()
    decay = tile4(-0.5 * inv)
    columns = []
    for u in (ux, uy, uz):
        w = grid - tile4(u)
        g = jnp.exp(w * w * decay)
        g1 = g * w
        g2 = g1 * w
        columns.append(jnp.concatenate([g, g1, g2, g2 * w], 1))
    sums = dot(table, jnp.concatenate(columns, 0))
    factors = []
    for axis, q in enumerate((qx, qy, qz)):
        kq = q * scale
        powers = []
        for power in range(4):
            row = 32 * axis + 8 * power
            t0, t1, t2, t3 = [sums[row : row + 8, CELLS * b : CELLS * (b + 1)] for b in range(4)]
            powers.append((t0, kq * t1, t2 * inv, kq * (t3 * inv - 5.0 * t1)))
        factors.append(powers)
    xs, ys, zs = factors
    pairs = {}

    def pair(ay, az):
        if (ay, az) not in pairs:
            y0, y1, y2, y3 = ys[ay]
            z0, z1, z2, z3 = zs[az]
            a = y0 * z0
            b = a + y3 * z0 + y0 * z3 + y1 * z2 + y2 * z1
            pairs[(ay, az)] = (a, b, y2 * z0 + y0 * z2, y1 * z0 + y0 * z1)
        return pairs[(ay, az)]

    out = []
    for terms in MOMENTS:
        total = 0.0
        for ax, ay, az in terms:
            x0, x1, x2, x3 = xs[ax]
            a, b, c, d = pair(ay, az)
            total = total + (x0 * b + x3 * a + x1 * c + x2 * d)
        out.append(pref * total)
    return out


def wall_moments(temp, tables):
    grid = speed_grid()
    g = jnp.exp(grid * grid * tile4(-0.5 / temp))
    sums = dot(tables, jnp.concatenate([g] * 3, 0))
    two_pi = 2.0 * np.pi * temp
    pref = box_volume / (two_pi * jnp.sqrt(two_pi))
    out = []
    for base in (0, 96):
        for terms in MOMENTS:
            total = 0.0
            for powers in terms:
                part = pref
                for axis in range(3):
                    row = base + 32 * axis + 8 * powers[axis]
                    part = part * sums[row : row + 8]
                total = total + part
            out.append(total)
    return out


def macro(m):
    m = [a * (1.0 / NV) for a in m]
    n = m[0]
    rn = 1.0 / n
    ux, uy, uz = m[1] * rn, m[2] * rn, m[3] * rn
    square = ux * ux + uy * uy + uz * uz
    energy = m[4] + m[5] + m[6]
    temp = (energy - n * square) * rn * (1.0 / 3.0)
    lift = 2.0 * n * square - energy
    qx = 0.5 * (m[10] + ux * lift) - (ux * m[4] + uy * m[7] + uz * m[8])
    qy = 0.5 * (m[11] + uy * lift) - (ux * m[7] + uy * m[5] + uz * m[9])
    qz = 0.5 * (m[12] + uz * lift) - (ux * m[8] + uy * m[9] + uz * m[6])
    rate = rate_field * n * jnp.exp(0.19 * jnp.log(temp))
    return (n, ux, uy, uz, temp, qx, qy, qz), rate


def spread(row):
    return jnp.broadcast_to(row, (8, CELLS))


def relax_params(m, table):
    params, rate = macro(m)
    for _ in range(2):
        s = [spread(a[:1]) for a in equilibrium_moments(params, table)]
        inv = 1.0 / (1.0 + rate)
        params, rate = macro([(a + rate * b) * inv for a, b in zip(m, s)])
    return params, rate


def here():
    x = lax.axis_index("space")
    p = lax.axis_index("z") * 4 + lax.axis_index("ylo") * 2 + lax.axis_index("core")
    return x, p


def half_start(index):
    return pl.multiple_of(index * HALF, HALF)


def split_kernel(f, fa, fb, sems):
    x, _ = here()
    odd = x % 2
    first = pltpu.make_async_copy(f.at[:, pl.ds(half_start(1 - odd), HALF)], fa, sems.at[0])
    second = pltpu.make_async_copy(f.at[:, pl.ds(half_start(odd), HALF)], fb, sems.at[1])
    first.start()
    second.start()
    first.wait()
    second.wait()


def setup_kernel(inflow, fb, temp_ref, type_ref, tables, infl, wa, wb, pre, wall, wall_bulk, cols, sems):
    x, p = here()
    odd = x % 2
    face = jnp.where(x >= 4, 1, 0)
    copy = pltpu.make_async_copy(inflow.at[face, :, pl.ds(half_start(1 - odd), HALF)], infl, sems.at[0])
    copy.start()
    cxd = speed_x(p)
    cy, cz = lane_speeds(p, 8)
    d = lax.broadcasted_iota(jnp.int32, (8, HALF), 0)
    common = jnp.where(d == 0, 1.0, 0.0)
    common = jnp.where(d == 3, courant * jnp.maximum(cy, 0.0), common)
    common = jnp.where(d == 4, courant * jnp.maximum(-cy, 0.0), common)
    common = jnp.where(d == 5, courant * jnp.maximum(cz, 0.0), common)
    common = jnp.where(d == 6, courant * jnp.maximum(-cz, 0.0), common)
    sign_a = jnp.where(odd == 0, 1.0, -1.0)
    for w, sign, row in ((wa, sign_a, 1 + odd), (wb, -sign_a, 2 - odd)):
        cx = sign * cxd
        multiplier = jnp.where(d == row, courant * cxd, common)
        ypow = [1.0, cy, cy * cy, cy * cy * cy]
        zpow = [1.0, cz, cz * cz, cz * cz * cz]
        xpow = [1.0, cx, cx * cx, cx * cx * cx]
        for k, terms in enumerate(MOMENTS):
            phi = 0.0
            for ax, ay, az in terms:
                phi = phi + xpow[ax] * (ypow[ay] * zpow[az])
            w[8 * k : 8 * k + 8, :] = multiplier * phi
        w[8 * NK : ROWS, :] = jnp.zeros((8, HALF), f32)
    edge = jnp.where(jnp.logical_or(x == 0, x == 7), 1.0, 0.0)
    sub = lax.broadcasted_iota(jnp.int32, (8, CELLS), 0)
    temp = jnp.broadcast_to(temp_ref[pl.ds(face, 1), :], (8, CELLS))
    kind = jnp.broadcast_to(type_ref[pl.ds(face, 1), :], (8, CELLS))
    for k, value in enumerate(wall_moments(temp, tables[face])):
        wall[8 * k : 8 * k + 8, :] = value
    two_pi = 2.0 * np.pi * temp
    rows = jnp.where(sub == 0, jnp.where(kind == 1, edge, 0.0), 0.0)
    rows = jnp.where(sub == 1, jnp.where(kind == 2, edge, 0.0), rows)
    rows = jnp.where(sub == 2, -0.5 / temp, rows)
    rows = jnp.where(sub == 3, box_volume / (two_pi * jnp.sqrt(two_pi)), rows)
    cols[...] = to_columns(rows)
    cy16, cz16 = lane_speeds(p, 16)
    speed_sq = cy16 * cy16 + cz16 * cz16 + cxd * cxd

    def step(i, carry):
        at = pl.ds(pl.multiple_of(i * 16, 16), 16)
        c = cols[at, :]
        wall_bulk[at, :] = c[:, 3:4] * jnp.exp(speed_sq * c[:, 2:3])
        return carry

    lax.fori_loop(0, 16, step, 0, unroll=4)
    flux = dot_t(jnp.full((8, HALF), 1.0, f32), fb[...]) * cxd
    pre[8 * NK : ROWS, :] = flux * edge
    copy.wait()
    in_rows = dot_t(wa[...], infl[...])
    for k in range(NK):
        pick = jnp.where(odd == 1, in_rows[8 * k + 2 : 8 * k + 3], in_rows[8 * k + 1 : 8 * k + 2])
        pre[8 * k : 8 * k + 8, :] = jnp.where(sub == 7, jnp.broadcast_to(pick, (8, CELLS)), 0.0) * edge


def upwind_y(p, i):
    return pl.ds(pl.multiple_of(((i + jnp.where(p % 2 == 1, 15, 1)) % 16) * 16, 16), 16)


def transport_weights(cxd, cy, cz):
    abs_y, abs_z = courant * jnp.abs(cy), courant * jnp.abs(cz)
    return 1.0 - courant * cxd - abs_y - abs_z, courant * cxd, abs_y, abs_z, cz > 0.0


def transport_block(value, neighbour_y, plane, weights):
    centre, abs_x, abs_y, abs_z, forward = weights
    neighbour_z = jnp.where(forward, pltpu.roll(value, 1, 0), pltpu.roll(value, 15, 0))
    return value * centre + abs_x * plane + abs_y * neighbour_y + abs_z * neighbour_z


def read_kernel(fa, fb, ha, hb, infl, cols, wa, wb, pre, ra, rb, keep, send):
    x, p = here()
    edge = jnp.where(jnp.logical_or(x == 0, x == 7), 1.0, 0.0)
    weights = transport_weights(speed_x(p), *lane_speeds(p, 16))

    def step(i, carry):
        at = pl.ds(pl.multiple_of(i * 16, 16), 16)
        up = upwind_y(p, i)
        c = cols[at, :]
        value = fa[at, :]
        plane = hb[at, :] * (1.0 - edge) + infl[at, :] * c[:, 0:1] + c[:, 1:2] * value
        ra[at, :] = transport_block(value, fa[up, :], plane, weights)
        rb[at, :] = transport_block(fb[at, :], fb[up, :], ha[at, :], weights)
        return carry

    lax.fori_loop(0, 16, step, 0, unroll=4)
    rows = pre[...] + dot_t(wa[...], ra[...]) + dot_t(wb[...], rb[...])
    north = p % 2 == 1
    top, bottom = rows[:HROWS], rows[HROWS:]
    keep[...] = jnp.where(north, bottom, top)
    send[...] = jnp.where(north, top, bottom)


def cell_kernel(mine, other, wall, type_ref, table, send_a, send_b, own, state):
    x, p = here()
    upper = x == 7
    odd = x % 2 == 1
    face = jnp.where(x >= 4, 1, 0)
    edge = jnp.where(jnp.logical_or(x == 0, upper), 1.0, 0.0)
    north = p % 2 == 1
    a, b = mine[...], other[...]
    rows = jnp.concatenate([jnp.where(north, b, a), jnp.where(north, a, b)], 0)
    m = [rows[8 * k : 8 * k + 8] for k in range(NK)]
    plain = [wall[8 * k : 8 * k + 8, :] for k in range(NK)]
    kind = jnp.broadcast_to(type_ref[pl.ds(face, 1), :], (8, CELLS))
    is_wall = jnp.where(kind == 0, edge, 0.0)
    is_in = jnp.where(kind == 1, edge, 0.0)
    is_out = jnp.where(kind == 2, edge, 0.0)

    def first(v):
        return jnp.where(odd, v[2:3], v[1:2])

    def second(v):
        return jnp.where(odd, v[1:2], v[2:3])

    entering = spread(first(plain[0])) * (1.0 / courant)
    amp = is_wall * spread(rows[8 * NK : 8 * NK + 1]) / entering
    inflow = [v[7:8] for v in m]
    m = [v + amp * wall[8 * (NK + k) : 8 * (NK + k) + 8, :] for k, v in enumerate(m)]
    params, rate = relax_params([spread(v[:1]) for v in m], table[...])
    s = equilibrium_moments(params, table[...])
    inv = 1.0 / (1.0 + rate)
    m = [(v + rate * w) * inv for v, w in zip(m, s)]
    amp2 = is_wall * spread(second(m[0])) * (1.0 / courant) / entering
    sub = lax.broadcasted_iota(jnp.int32, (8, CELLS), 0)
    lane = lax.broadcasted_iota(jnp.int32, (8, CELLS), 1)
    low, high = lane % 16 == 0, lane % 16 == 15
    for k in range(NK):
        v = m[k]
        z_up = jnp.where(low, pltpu.roll(v, CELLS - 15, 1), pltpu.roll(v, 1, 1))
        z_down = jnp.where(high, pltpu.roll(v, 15, 1), pltpu.roll(v, CELLS - 1, 1))
        total = jnp.where(sub == 0, v, jnp.where(sub == 7, 0.0, -v))
        total = total + jnp.where(sub == 3, pltpu.roll(v, 16, 1), 0.0)
        total = total + jnp.where(sub == 4, pltpu.roll(v, CELLS - 16, 1), 0.0)
        total = total + jnp.where(sub == 5, z_up, 0.0) + jnp.where(sub == 6, z_down, 0.0)
        va = first(v)
        ghost = amp2[:1] * first(plain[k]) + is_in[:1] * inflow[k] + is_out[:1] * va
        own[k : k + 1, :] = jnp.sum(total, 0, keepdims=True) + ghost
        send_a[k : k + 1, :] = va
        send_b[k : k + 1, :] = second(v)
    own[NK:16, :] = jnp.zeros((3, CELLS), f32)
    extra = list(params) + [rate, amp]
    for k, v in enumerate(extra):
        send_a[NK + k : NK + k + 1, :] = v[:1]
        send_b[NK + k : NK + k + 1, :] = v[:1]
        state[k : k + 1, :] = v[:1]
    send_a[23:24, :] = jnp.zeros((1, CELLS), f32)
    send_b[23:24, :] = jnp.zeros((1, CELLS), f32)
    state[10:11, :] = amp2[:1]
    state[11:16, :] = jnp.zeros((5, CELLS), f32)


NCOL = 16


def bulk_rows(params, rate, cx_a, cx_b, extra=()):
    n, ux, uy, uz, temp, qx, qy, qz = params
    inv = 1.0 / temp
    two_pi = 2.0 * np.pi * temp
    share = 1.0 / (1.0 + rate)
    scale = inv * inv / (15.0 * n)
    pref = rate * share * n * box_volume / (two_pi * jnp.sqrt(two_pi))
    rows = [uy, uz, -0.5 * inv, inv, qy * scale, qz * scale, share]
    for cx in (cx_a, cx_b):
        w = cx - ux
        square = w * w
        rows += [pref * jnp.exp(-0.5 * inv * square), qx * scale * w, square * inv]
    rows += list(extra)
    return rows + [jnp.zeros((1, CELLS), f32)] * (NCOL - len(rows))


def columns(c, base):
    return [c[:, base + j : base + j + 1] for j in range(NCOL)]


def shared_part(k, cy, cz):
    wy = cy - k[0]
    wz = cz - k[1]
    square = wy * wy + wz * wz
    return jnp.exp(square * k[2]), square * k[3] - 5.0, wy * k[4] + wz * k[5]


def relaxed(value, k, part, half):
    decay, square, heat = part
    pref, heat_x, square_x = k[7 + 3 * half : 10 + 3 * half]
    return value * k[6] + (decay * pref) * (1.0 + (heat + heat_x) * (square + square_x))


def own_kernel(ra, rb, state, wall_bulk, ca, cb, work):
    x, p = here()
    cxd = speed_x(p)
    sign_a = jnp.where(x % 2 == 0, 1.0, -1.0)
    cy, cz = lane_speeds(p, 16)
    st = state[...]
    rows = bulk_rows(
        [st[k : k + 1] for k in range(8)], st[8:9], sign_a * cxd, -sign_a * cxd, [st[9:10] * (courant * cxd)]
    )
    work[...] = to_columns(jnp.concatenate(rows, 0))

    def step(i, carry):
        at = pl.ds(pl.multiple_of(i * 16, 16), 16)
        k = columns(work[at, :], 0)
        part = shared_part(k, cy, cz)
        ca[at, :] = relaxed(ra[at, :] + k[13] * wall_bulk[at, :], k, part, 0)
        cb[at, :] = relaxed(rb[at, :], k, part, 1)
        return carry

    lax.fori_loop(0, 16, step, 0, unroll=4)


def final_kernel(
    ca, cb, ha, hb, from_a, from_b, own, state, wall_bulk, infl, cols, table, out, fields, pa, pb, oa, ob, work, sems
):
    x, p = here()
    odd = x % 2
    cxd = speed_x(p)
    sign_a = jnp.where(odd == 0, 1.0, -1.0)
    cx_a, cx_b = sign_a * cxd, -sign_a * cxd
    cy, cz = lane_speeds(p, 16)
    weights = transport_weights(cxd, cy, cz)
    edge = jnp.where(jnp.logical_or(x == 0, x == 7), 1.0, 0.0)
    ta, tb, st = from_a[...], from_b[...], state[...]
    m = [spread(own[k : k + 1, :] + ta[k : k + 1] + tb[k : k + 1]) for k in range(NK)]
    params, rate = relax_params(m, table[...])
    wall_scale = courant * cxd
    tb = jnp.where(edge > 0.0, st[:10], tb[NK : NK + 10])
    ta = ta[NK : NK + 10]

    def coefficients(source, extra=()):
        return bulk_rows([source[k : k + 1] for k in range(8)], source[8:9], cx_a, cx_b, extra)

    rows = coefficients(ta, [ta[9:10] * wall_scale])
    rows += coefficients(tb, [jnp.zeros((1, CELLS), f32), st[10:11]])
    rows += bulk_rows([v[:1] for v in params], rate[:1], cx_a, cx_b)
    work[...] = to_columns(jnp.concatenate(rows, 0))

    def first(i, carry):
        at = pl.ds(pl.multiple_of(i * 16, 16), 16)
        c = work[at, :]
        k = cols[at, :]
        w = wall_bulk[at, :]
        ka, kb = columns(c, 0), columns(c, NCOL)
        halo = relaxed(hb[at, :], kb, shared_part(kb, cy, cz), 0)
        pa[at, :] = (1.0 - edge) * halo + infl[at, :] * k[:, 0:1] + kb[14] * w + k[:, 1:2] * ca[at, :]
        pb[at, :] = relaxed(ha[at, :] + ka[13] * w, ka, shared_part(ka, cy, cz), 1)
        return carry

    lax.fori_loop(0, 16, first, 0, unroll=4)
    copies = []
    for chunk in range(4):

        def second(i, carry):
            at = pl.ds(pl.multiple_of(i * 16, 16), 16)
            up = upwind_y(p, i)
            k = columns(work[at, :], 2 * NCOL)
            part = shared_part(k, cy, cz)
            read = transport_block(ca[at, :], ca[up, :], pa[at, :], weights)
            oa[at, :] = relaxed(read, k, part, 0)
            read = transport_block(cb[at, :], cb[up, :], pb[at, :], weights)
            ob[at, :] = relaxed(read, k, part, 1)
            return carry

        lax.fori_loop(4 * chunk, 4 * chunk + 4, second, 0, unroll=4)
        at = pl.ds(64 * chunk, 64)
        for half, source, start in ((0, oa, 1 - odd), (1, ob, odd)):
            copy = pltpu.make_async_copy(
                source.at[at, :], out.at[at, pl.ds(half_start(start), HALF)], sems.at[2 * chunk + half]
            )
            copy.start()
            copies.append(copy)
    table8 = jnp.concatenate([v[:1] for v in params], 0)
    for y in range(16):
        fields[:, y, :] = table8[:, 16 * y : 16 * y + 16]
    for copy in copies:
        copy.wait()


VMEM = pl.BlockSpec(memory_space=pltpu.VMEM)
ANY = pl.BlockSpec(memory_space=pl.ANY)
PLANE = (CELLS, HALF)


def call(kernel, outs, args, scratch=(), sems=0, loose_in=(), loose_out=(), cost=1_000_000, grant=16):
    scratches = [pltpu.VMEM(s, f32) for s in scratch]
    if sems:
        scratches.append(pltpu.SemaphoreType.DMA((sems,)))
    return pl.pallas_call(
        kernel,
        out_shape=[jax.ShapeDtypeStruct(s, f32) for s in outs],
        in_specs=[ANY if k in loose_in else VMEM for k in range(len(args))],
        out_specs=[ANY if k in loose_out else VMEM for k in range(len(outs))],
        scratch_shapes=scratches,
        cost_estimate=pl.CostEstimate(flops=cost, bytes_accessed=1 << 20, transcendentals=0),
        compiler_params=pltpu.CompilerParams(vmem_limit_bytes=grant << 20),
    )(*args)


PAIRS_A = [(i, i ^ 1) for i in range(8)]
PAIRS_B = [pair for i in (1, 3, 5) for pair in ((i, i + 1), (i + 1, i))]
SWAP = [(0, 1), (1, 0)]


def both_ways(pairs):
    return [pair for i, j in pairs for pair in ((i, j), (j, i))]


Z_ROUNDS = [
    ("zround1", both_ways([(0, 1), (2, 3), (4, 5), (6, 7)])),
    ("zround2", both_ways([(0, 2), (1, 3), (4, 6), (5, 7)])),
    ("zround3", both_ways([(0, 6), (1, 7), (2, 4), (3, 5)])),
]


def swap_planes(a, b):
    b = lax.ppermute(b, "space", PAIRS_B)
    a = lax.ppermute(a, "space", PAIRS_A)
    return a, b


def body(distribution, inflow, wall_temp, face_type):
    f = distribution.reshape(CELLS, 2 * HALF)
    fa, fb = call(split_kernel, [PLANE, PLANE], [f], sems=2, loose_in=(0,))
    ha, hb = swap_planes(fa, fb)
    temp = wall_temp.reshape(2, CELLS)
    kind = face_type.reshape(2, CELLS)
    table = jnp.asarray(TABLE)
    infl, wa, wb, pre, wall, wall_bulk, cols = call(
        setup_kernel,
        [PLANE, (ROWS, HALF), (ROWS, HALF), (ROWS, CELLS), (2 * NK * 8, CELLS), PLANE, (CELLS, 128)],
        [inflow.reshape(2, CELLS, 2 * HALF), fb, temp, kind, jnp.asarray(WALL_TABLES)],
        sems=1,
        loose_in=(0,),
    )
    ra, rb, keep, send = call(
        read_kernel,
        [PLANE, PLANE, (HROWS, CELLS), (HROWS, CELLS)],
        [fa, fb, ha, hb, infl, cols, wa, wb, pre],
    )
    part = keep + lax.ppermute(send, "core", SWAP)
    part = part + lax.ppermute(part, "ylo", SWAP)
    ga = lax.optimization_barrier((ra, part))[0]
    gb = rb
    for name, pairs in Z_ROUNDS:
        if name == "zround2":
            gb = lax.optimization_barrier((rb, part))[0]
        part = part + lax.ppermute(part, "z", pairs)
    ga, gb = swap_planes(ga, gb)
    other = lax.ppermute(part, "core", SWAP)
    send_a, send_b, own, state = call(
        cell_kernel,
        [(24, CELLS), (24, CELLS), (16, CELLS), (16, CELLS)],
        [part, other, wall, kind, table],
    )
    from_a, from_b = swap_planes(send_a, send_b)
    ca, cb = call(own_kernel, [PLANE, PLANE], [ra, rb, state, wall_bulk], scratch=[(CELLS, 128)], cost=40_000_000)
    out, fields = call(
        final_kernel,
        [(CELLS, 2 * HALF), (8, 16, 16)],
        [ca, cb, ga, gb, from_a, from_b, own, state, wall_bulk, infl, cols, table],
        scratch=[PLANE] * 4 + [(CELLS, 128)],
        sems=8,
        loose_out=(0,),
    )
    return out.reshape(1, 16, 16, 2 * HALF), fields[:, None]


def solution(mesh):
    split = Mesh(mesh.devices.reshape(8, 8, 2, 2), ("space", "z", "ylo", "core"))
    vel = ("z", "ylo", "core")
    in_specs = (P("space", None, None, vel), P(None, None, None, vel), P(), P())
    out_specs = (P("space", None, None, vel), P(None, "space", None, None))

    return jax.shard_map(body, mesh=split, in_specs=in_specs, out_specs=out_specs, check_vma=False)
```

profile of v0, /device:TPU:38, one launch (start us, length us, event | category | flops | bytes accessed | tf_op | source)
XLA Modules:
  0.0 71.7 jit_solution(6197774336612615211)
XLA Ops:
  0.6 0.0 copy-start.1
  0.6 1.2 %copy-done.1 = f32[1,16,16,1024]{3,2,1,0:T(8,128)S(1)} copy-done((f32[1,16,16,1024]{3,2,1,0:T(8,128)S(1)}, f32[1,16,16,1024]{3,2,1,0:T(8,128)}, u32[]{:S(2)}) %copy-start.1) | copy-done | bytes 1048600
  1.9 0.1 shard_map.77
  2.0 0.9 %collective-permute-start = (f32[256,512]{1,0:T(8,128)S(1)}, f32[256,512]{1,0:T(8,128)S(1)}, u32[]{:S(2)}, u32[]{:S(2)}) collective-permute-start(f32[256,512]{1,0:T(8,128)S(1)} %get-tuple-element.25.fa), channel_id=1, source_target_pairs={{0,32},{32,0},{64,96},{96,64},{128,160},{160,128},{192,224},{224,1... | collective-permute-start | bytes 1572872 | tf_op jit(solution)/shard_map/ppermute | solution.py:531
  2.9 5.7 %collective-permute-start.1 = (f32[256,512]{1,0:T(8,128)S(1)}, f32[256,512]{1,0:T(8,128)S(1)}, u32[]{:S(2)}, u32[]{:S(2)}) collective-permute-start(f32[256,512]{1,0:T(8,128)S(1)} %get-tuple-element.26.fb), channel_id=1, source_target_pairs={{32,64},{64,32},{96,128},{128,96},{160,192},{192,160},{33,65},{65,... | collective-permute-start | bytes 1572872 | tf_op jit(solution)/shard_map/ppermute | solution.py:530
  8.6 0.8 %reshape.22.type_ref = s32[2,256]{1,0:T(2,128)S(1)} reshape(s32[2,16,16]{2,1,0:T(8,128)} %param.9) | data formatting | bytes 4096 | tf_op jit(solution)/shard_map/reshape | solution.py:540
  9.4 0.8 %reshape.21.temp_ref = f32[2,256]{1,0:T(2,128)S(1)} reshape(f32[2,16,16]{2,1,0:T(8,128)} %param.8) | data formatting | bytes 4096 | tf_op jit(solution)/shard_map/reshape | solution.py:539
  10.2 0.0 copy-start
  10.2 1.6 %copy-done = f32[2,16,16,1024]{3,2,1,0:T(8,128)S(1)} copy-done((f32[2,16,16,1024]{3,2,1,0:T(8,128)S(1)}, f32[2,16,16,1024]{3,2,1,0:T(8,128)}, u32[]{:S(2)}) %copy-start) | copy-done | bytes 2097176
  11.8 0.0 copy-start.2
  11.8 0.9 %copy-done.2 = f32[2,192,96]{2,1,0:T(8,128)S(1)} copy-done((f32[2,192,96]{2,1,0:T(8,128)S(1)}, f32[2,192,96]{2,1,0:T(8,128)}, u32[]{:S(2)}) %copy-start.2) | copy-done | bytes 147480
  12.7 2.6 %shard_map.78 = (f32[256,512]{1,0:T(8,128)S(1)}, f32[112,512]{1,0:T(8,128)S(1)}, f32[112,512]{1,0:T(8,128)S(1)}, f32[112,256]{1,0:T(8,128)S(1)}, f32[208,256]{1,...) custom-call(f32[2,256,1024]{2,1,0:T(8,128)S(1)} %bitcast.6, f32[256,512]{1,0:T(8,128)S(1)} %get-tuple-element.26.fb, ...), custom_call_target="tpu_custom_call" | custom-call | flops 1000000 | bytes 1048576 | tf_op jit(solution)/shard_map/pallas_call | solution.py:502
  15.3 0.4 collective-permute-done.ha
  15.7 6.0 %collective-permute-done.1.hb = f32[256,512]{1,0:T(8,128)S(1)} collective-permute-done((f32[256,512]{1,0:T(8,128)S(1)}, f32[256,512]{1,0:T(8,128)S(1)}, u32[]{:S(2)}, u32[]{:S(2)}) %collective-permute-start.1) | collective-permute-done | bytes 524320 | tf_op jit(solution)/shard_map/ppermute | solution.py:530
  21.8 0.0 copy-start.3
  21.8 1.8 %shard_map.79 = (f32[256,512]{1,0:T(8,128)S(1)}, f32[256,512]{1,0:T(8,128)S(1)}, f32[56,256]{1,0:T(8,128)S(1)}, f32[56,256]{1,0:T(8,128)S(1)}) custom-call(f32[256,512]{1,0:T(8,128)S(1)} %get-tuple-element.25.fa, f32[256,512]{1,0:T(8,128)S(1)} %get-tuple-element.26.fb, f32[256,512]{1,0:T(8,128)S(1)} %collective-permute-done.ha, ...), custom_call_target="tpu_custom_call" | custom-call | flops 1000000 | bytes 1048576 | tf_op jit(solution)/shard_map/pallas_call | solution.py:502
  23.6 0.1 collective-permute-start.2
  23.7 1.2 %collective-permute-done.2 = f32[56,256]{1,0:T(8,128)S(1)} collective-permute-done((f32[56,256]{1,0:T(8,128)S(1)}, f32[56,256]{1,0:T(8,128)S(1)}, u32[]{:S(2)}, u32[]{:S(2)}) %collective-permute-start.2) | collective-permute-done | bytes 57376 | tf_op jit(solution)/shard_map/ppermute | solution.py:554
  24.9 1.7 %collective-permute-start.3 = (f32[56,256]{1,0:T(8,128)S(1)}, f32[56,256]{1,0:T(8,128)S(1)}, u32[]{:S(2)}, u32[]{:S(2)}) collective-permute-start(f32[56,256]{1,0:T(8,128)S(1)} %add.15), channel_id=1, source_target_pairs={{0,2},{2,0},{1,3},{3,1},{4,6},{6,4},{5,7},{7,5},{8,10},{10,8},{9,1... | collective-permute-start | bytes 172040 | tf_op jit(solution)/shard_map/ppermute | solution.py:555
  26.6 2.6 %collective-permute-done.3 = f32[56,256]{1,0:T(8,128)S(1)} collective-permute-done((f32[56,256]{1,0:T(8,128)S(1)}, f32[56,256]{1,0:T(8,128)S(1)}, u32[]{:S(2)}, u32[]{:S(2)}) %collective-permute-start.3) | collective-permute-done | bytes 57376 | tf_op jit(solution)/shard_map/ppermute | solution.py:555
  29.2 0.2 collective-permute-start.4
  29.4 0.0 collective-permute-start.8
  29.4 4.1 %collective-permute-done.4 = f32[56,256]{1,0:T(8,128)S(1)} collective-permute-done((f32[56,256]{1,0:T(8,128)S(1)}, f32[56,256]{1,0:T(8,128)S(1)}, u32[]{:S(2)}, u32[]{:S(2)}) %collective-permute-start.4) | collective-permute-done | bytes 57376 | tf_op jit(solution)/shard_map/ppermute | solution.py:561
  33.5 5.8 %collective-permute-start.9 = (f32[256,512]{1,0:T(8,128)S(1)}, f32[256,512]{1,0:T(8,128)S(1)}, u32[]{:S(2)}, u32[]{:S(2)}) collective-permute-start(f32[256,512]{1,0:T(8,128)S(1)} %get-tuple-element.42.rb), channel_id=1, source_target_pairs={{32,64},{64,32},{96,128},{128,96},{160,192},{192,160},{33,65},{65,... | collective-permute-start | bytes 1572872 | tf_op jit(solution)/shard_map/ppermute | solution.py:530
  39.2 3.4 %collective-permute-start.5 = (f32[56,256]{1,0:T(8,128)S(1)}, f32[56,256]{1,0:T(8,128)S(1)}, u32[]{:S(2)}, u32[]{:S(2)}) collective-permute-start(f32[56,256]{1,0:T(8,128)S(1)} %add.17), channel_id=1, source_target_pairs={{0,8},{8,0},{4,12},{12,4},{16,24},{24,16},{20,28},{28,20},{1,9},{9... | collective-permute-start | bytes 172040 | tf_op jit(solution)/shard_map/ppermute | solution.py:561
  42.6 2.2 %collective-permute-done.5 = f32[56,256]{1,0:T(8,128)S(1)} collective-permute-done((f32[56,256]{1,0:T(8,128)S(1)}, f32[56,256]{1,0:T(8,128)S(1)}, u32[]{:S(2)}, u32[]{:S(2)}) %collective-permute-start.5) | collective-permute-done | bytes 57376 | tf_op jit(solution)/shard_map/ppermute | solution.py:561
  44.8 5.8 %collective-permute-start.6 = (f32[56,256]{1,0:T(8,128)S(1)}, f32[56,256]{1,0:T(8,128)S(1)}, u32[]{:S(2)}, u32[]{:S(2)}) collective-permute-start(f32[56,256]{1,0:T(8,128)S(1)} %add.18), channel_id=1, source_target_pairs={{0,24},{24,0},{4,28},{28,4},{8,16},{16,8},{12,20},{20,12},{1,25},{... | collective-permute-start | bytes 172040 | tf_op jit(solution)/shard_map/ppermute | solution.py:561
  50.5 2.7 %collective-permute-done.6 = f32[56,256]{1,0:T(8,128)S(1)} collective-permute-done((f32[56,256]{1,0:T(8,128)S(1)}, f32[56,256]{1,0:T(8,128)S(1)}, u32[]{:S(2)}, u32[]{:S(2)}) %collective-permute-start.6) | collective-permute-done | bytes 57376 | tf_op jit(solution)/shard_map/ppermute | solution.py:561
  53.2 0.1 collective-permute-start.7
  53.3 1.2 %collective-permute-done.7.other = f32[56,256]{1,0:T(8,128)S(1)} collective-permute-done((f32[56,256]{1,0:T(8,128)S(1)}, f32[56,256]{1,0:T(8,128)S(1)}, u32[]{:S(2)}, u32[]{:S(2)}) %collective-permute-start.7) | collective-permute-done | bytes 57376 | tf_op jit(solution)/shard_map/ppermute | solution.py:563
  54.6 0.0 copy-done.3
  54.6 2.0 %shard_map.80 = (f32[24,256]{1,0:T(8,128)S(1)}, f32[24,256]{1,0:T(8,128)S(1)}, f32[16,256]{1,0:T(8,128)S(1)}, f32[16,256]{1,0:T(8,128)S(1)}) custom-call(f32[56,256]{1,0:T(8,128)S(1)} %add.19.mine, f32[56,256]{1,0:T(8,128)S(1)} %collective-permute-done.7.other, f32[208,256]{1,0:T(8,128)S(1)} %get-tuple-element.36.wall, s32[2,256]{1,0:T(2,128)S(1)} %reshape.22.type_ref, ...), custom_call_target="tpu_custom_call" | custom-call | flops 1000000 | bytes 1048576 | tf_op jit(solution)/shard_map/pallas_call | solution.py:502
  56.6 0.1 collective-permute-start.10
  56.7 3.9 %collective-permute-start.11 = (f32[24,256]{1,0:T(8,128)S(1)}, f32[24,256]{1,0:T(8,128)S(1)}, u32[]{:S(2)}, u32[]{:S(2)}) collective-permute-start(f32[24,256]{1,0:T(8,128)S(1)} %get-tuple-element.44), channel_id=1, source_target_pairs={{32,64},{64,32},{96,128},{128,96},{160,192},{192,160},{33,65},{65,... | collective-permute-start | bytes 73736 | tf_op jit(solution)/shard_map/ppermute | solution.py:530
  60.5 1.2 %shard_map.81 = (f32[256,512]{1,0:T(8,128)S(1)}, f32[256,512]{1,0:T(8,128)S(1)}) custom-call(f32[256,512]{1,0:T(8,128)S(1)} %get-tuple-element.41.ra, f32[256,512]{1,0:T(8,128)S(1)} %get-tuple-element.42.rb, f32[16,256]{1,0:T(8,128)S(1)} %get-tuple-element.37.state, f32[256,512]{1,0:T(8,128)S(1)} %get-tuple-element.38.wall_bulk), custom_call_target="tpu_custom_call" | custom-call | flops 40000000 | bytes 1048576 | tf_op jit(solution)/shard_map/pallas_call | solution.py:502
  61.7 0.0 collective-permute-done.10.from_a
  61.7 4.3 %collective-permute-done.11.from_b = f32[24,256]{1,0:T(8,128)S(1)} collective-permute-done((f32[24,256]{1,0:T(8,128)S(1)}, f32[24,256]{1,0:T(8,128)S(1)}, u32[]{:S(2)}, u32[]{:S(2)}) %collective-permute-start.11) | collective-permute-done | bytes 24608 | tf_op jit(solution)/shard_map/ppermute | solution.py:530
  66.0 0.0 collective-permute-done.8.ha
  66.0 0.0 collective-permute-done.9.hb
  66.0 5.5 %shard_map.82 = (f32[256,1024]{1,0:T(8,128)}, f32[8,16,16]{2,1,0:T(8,128)}) custom-call(f32[256,512]{1,0:T(8,128)S(1)} %get-tuple-element.39.ca, f32[256,512]{1,0:T(8,128)S(1)} %get-tuple-element.40.cb, f32[256,512]{1,0:T(8,128)S(1)} %collective-permute-done.8.ha, f32[256,512]{1,0:T(8,128)S(1)} %collective-permute-done.9.hb, ...), custom_call_target="tpu_custom_call" | custom-call | flops 1000000 | bytes 1048576 | tf_op jit(solution)/shard_map/pallas_call | solution.py:502
  (5 shorter events, 0.0 us)
Async XLA Ops:
  0.6 1.2 %copy-start.1 = (f32[1,16,16,1024]{3,2,1,0:T(8,128)S(1)}, f32[1,16,16,1024]{3,2,1,0:T(8,128)}, u32[]{:S(2)}) copy-start(f32[1,16,16,1024]{3,2,1,0:T(8,128)} %param.6) | copy-start | bytes 3145732
  2.0 13.8 %collective-permute-start = (f32[256,512]{1,0:T(8,128)S(1)}, f32[256,512]{1,0:T(8,128)S(1)}, u32[]{:S(2)}, u32[]{:S(2)}) collective-permute-start(f32[256,512]{1,0:T(8,128)S(1)} %get-tuple-element.25.fa), channel_id=1, source_target_pairs={{0,32},{32,0},{64,96},{96,64},{128,160},{160,128},{192,224},{224,1... | collective-permute-start | bytes 1572872 | tf_op jit(solution)/shard_map/ppermute | solution.py:531
  2.9 18.9 %collective-permute-start.1 = (f32[256,512]{1,0:T(8,128)S(1)}, f32[256,512]{1,0:T(8,128)S(1)}, u32[]{:S(2)}, u32[]{:S(2)}) collective-permute-start(f32[256,512]{1,0:T(8,128)S(1)} %get-tuple-element.26.fb), channel_id=1, source_target_pairs={{32,64},{64,32},{96,128},{128,96},{160,192},{192,160},{33,65},{65,... | collective-permute-start | bytes 1572872 | tf_op jit(solution)/shard_map/ppermute | solution.py:530
  10.2 1.6 %copy-start = (f32[2,16,16,1024]{3,2,1,0:T(8,128)S(1)}, f32[2,16,16,1024]{3,2,1,0:T(8,128)}, u32[]{:S(2)}) copy-start(f32[2,16,16,1024]{3,2,1,0:T(8,128)} %param.7) | copy-start | bytes 6291460
  11.8 0.9 %copy-start.2 = (f32[2,192,96]{2,1,0:T(8,128)S(1)}, f32[2,192,96]{2,1,0:T(8,128)}, u32[]{:S(2)}) copy-start(f32[2,192,96]{2,1,0:T(8,128)} %constant.5.clone.tables) | copy-start | bytes 442372
  21.8 32.8 %copy-start.3 = (f32[96,96]{1,0:T(8,128)S(1)}, f32[96,96]{1,0:T(8,128)}, u32[]{:S(2)}) copy-start(f32[96,96]{1,0:T(8,128)} %constant.4.clone.table) | copy-start | bytes 110596
  23.6 1.3 %collective-permute-start.2 = (f32[56,256]{1,0:T(8,128)S(1)}, f32[56,256]{1,0:T(8,128)S(1)}, u32[]{:S(2)}, u32[]{:S(2)}) collective-permute-start(f32[56,256]{1,0:T(8,128)S(1)} %get-tuple-element.35), channel_id=1, source_target_pairs={{0,1},{1,0},{2,3},{3,2},{4,5},{5,4},{6,7},{7,6},{8,9},{9,8},{10,11... | collective-permute-start | bytes 172040 | tf_op jit(solution)/shard_map/ppermute | solution.py:554
  24.9 4.3 %collective-permute-start.3 = (f32[56,256]{1,0:T(8,128)S(1)}, f32[56,256]{1,0:T(8,128)S(1)}, u32[]{:S(2)}, u32[]{:S(2)}) collective-permute-start(f32[56,256]{1,0:T(8,128)S(1)} %add.15), channel_id=1, source_target_pairs={{0,2},{2,0},{1,3},{3,1},{4,6},{6,4},{5,7},{7,5},{8,10},{10,8},{9,1... | collective-permute-start | bytes 172040 | tf_op jit(solution)/shard_map/ppermute | solution.py:555
  29.2 4.3 %collective-permute-start.4 = (f32[56,256]{1,0:T(8,128)S(1)}, f32[56,256]{1,0:T(8,128)S(1)}, u32[]{:S(2)}, u32[]{:S(2)}) collective-permute-start(f32[56,256]{1,0:T(8,128)S(1)} %add.16), channel_id=1, source_target_pairs={{0,4},{4,0},{8,12},{12,8},{16,20},{20,16},{24,28},{28,24},{1,5},{5... | collective-permute-start | bytes 172040 | tf_op jit(solution)/shard_map/ppermute | solution.py:561
  29.4 36.6 %collective-permute-start.8 = (f32[256,512]{1,0:T(8,128)S(1)}, f32[256,512]{1,0:T(8,128)S(1)}, u32[]{:S(2)}, u32[]{:S(2)}) collective-permute-start(f32[256,512]{1,0:T(8,128)S(1)} %get-tuple-element.41.ra), channel_id=1, source_target_pairs={{0,32},{32,0},{64,96},{96,64},{128,160},{160,128},{192,224},{224,1... | collective-permute-start | bytes 1572872 | tf_op jit(solution)/shard_map/ppermute | solution.py:531
  33.5 32.6 %collective-permute-start.9 = (f32[256,512]{1,0:T(8,128)S(1)}, f32[256,512]{1,0:T(8,128)S(1)}, u32[]{:S(2)}, u32[]{:S(2)}) collective-permute-start(f32[256,512]{1,0:T(8,128)S(1)} %get-tuple-element.42.rb), channel_id=1, source_target_pairs={{32,64},{64,32},{96,128},{128,96},{160,192},{192,160},{33,65},{65,... | collective-permute-start | bytes 1572872 | tf_op jit(solution)/shard_map/ppermute | solution.py:530
  39.2 5.5 %collective-permute-start.5 = (f32[56,256]{1,0:T(8,128)S(1)}, f32[56,256]{1,0:T(8,128)S(1)}, u32[]{:S(2)}, u32[]{:S(2)}) collective-permute-start(f32[56,256]{1,0:T(8,128)S(1)} %add.17), channel_id=1, source_target_pairs={{0,8},{8,0},{4,12},{12,4},{16,24},{24,16},{20,28},{28,20},{1,9},{9... | collective-permute-start | bytes 172040 | tf_op jit(solution)/shard_map/ppermute | solution.py:561
  44.8 8.5 %collective-permute-start.6 = (f32[56,256]{1,0:T(8,128)S(1)}, f32[56,256]{1,0:T(8,128)S(1)}, u32[]{:S(2)}, u32[]{:S(2)}) collective-permute-start(f32[56,256]{1,0:T(8,128)S(1)} %add.18), channel_id=1, source_target_pairs={{0,24},{24,0},{4,28},{28,4},{8,16},{16,8},{12,20},{20,12},{1,25},{... | collective-permute-start | bytes 172040 | tf_op jit(solution)/shard_map/ppermute | solution.py:561
  53.2 1.3 %collective-permute-start.7 = (f32[56,256]{1,0:T(8,128)S(1)}, f32[56,256]{1,0:T(8,128)S(1)}, u32[]{:S(2)}, u32[]{:S(2)}) collective-permute-start(f32[56,256]{1,0:T(8,128)S(1)} %add.19.mine), channel_id=1, source_target_pairs={{0,1},{1,0},{2,3},{3,2},{4,5},{5,4},{6,7},{7,6},{8,9},{9,8},{10,11... | collective-permute-start | bytes 172040 | tf_op jit(solution)/shard_map/ppermute | solution.py:563
  56.6 5.2 %collective-permute-start.10 = (f32[24,256]{1,0:T(8,128)S(1)}, f32[24,256]{1,0:T(8,128)S(1)}, u32[]{:S(2)}, u32[]{:S(2)}) collective-permute-start(f32[24,256]{1,0:T(8,128)S(1)} %get-tuple-element.43), channel_id=1, source_target_pairs={{0,32},{32,0},{64,96},{96,64},{128,160},{160,128},{192,224},{224,1... | collective-permute-start | bytes 73736 | tf_op jit(solution)/shard_map/ppermute | solution.py:531
  56.7 9.3 %collective-permute-start.11 = (f32[24,256]{1,0:T(8,128)S(1)}, f32[24,256]{1,0:T(8,128)S(1)}, u32[]{:S(2)}, u32[]{:S(2)}) collective-permute-start(f32[24,256]{1,0:T(8,128)S(1)} %get-tuple-element.44), channel_id=1, source_target_pairs={{32,64},{64,32},{96,128},{128,96},{160,192},{192,160},{33,65},{65,... | collective-permute-start | bytes 73736 | tf_op jit(solution)/shard_map/ppermute | solution.py:530
where the time goes:
time: 72.1 us; the launch traced here: 71.7 us
  starting transfers between devices  27.5 us (38%)
  waiting for transfers between devices  24.7 us (34%)
  Pallas kernels  13.2 us (18%)
  local copies, waits for them, and re-layouts  5.34 us (7%)
  between operations  0.91 us (1%)
    ppermute x3, starting transfers between devices, swap_planes(): b = lax.ppermute(b, 'space', PAIRS_B)  15.3 us
    pallas_call x6, Pallas kernels, call(): pl.pallas_call(kernel, out_shape=[jax.ShapeDtypeStruct(s, f32) for s in o...  13.2 us
    ppermute x3, waiting for transfers between devices, swap_planes(): b = lax.ppermute(b, 'space', PAIRS_B)  10.3 us
    ppermute x3, starting transfers between devices, body(): part = part + lax.ppermute(part, 'z', pairs)  9.3 us
    ppermute x3, waiting for transfers between devices, body(): part = part + lax.ppermute(part, 'z', pairs)  8.93 us
    unnamed x8, local copies, waits for them, and re-layouts  3.74 us
    ppermute x1, waiting for transfers between devices, body(): part = part + lax.ppermute(part, 'ylo', SWAP)  2.6 us
    ppermute x1, starting transfers between devices, body(): part = part + lax.ppermute(part, 'ylo', SWAP)  1.66 us
  transfers between devices with their start and end apart: 12, of which 9 were waited for; matrix products, arithmetic and copies ran while one was open for 2% of the time, Pallas kernels for 8%

commit v1 on v0

--- a/solution.py
+++ b/solution.py
@@ -11,7 +11,7 @@
 CELLS = 256
 HALF = 512
 NK = 13
-ROWS = 112
+ROWS = 96
 HROWS = ROWS // 2
 courant = 0.08
 rate_field = 0.8
@@ -36,28 +36,35 @@
 ]
 
 
-def axis_tables():
+def axis_table(top):
     grid = (np.arange(32) + 0.5) * 0.25 - 4.0
     plus, minus = courant * np.maximum(grid, 0.0), courant * np.maximum(-grid, 0.0)
-    table = np.zeros((96, 96))
+    table = np.zeros((24 * top, 96))
     for axis in range(3):
-        for power in range(4):
+        for power in range(top):
             for d in range(7):
                 row = grid**power
                 if d == 1 + 2 * axis:
                     row = row * plus
                 if d == 2 + 2 * axis:
                     row = row * minus
-                table[32 * axis + 8 * power + d, 32 * axis : 32 * axis + 32] = row
+                table[8 * top * axis + 8 * power + d, 32 * axis : 32 * axis + 32] = row
+    return table.astype(np.float32), plus, minus
+
+
+def wall_tables():
+    table, plus, minus = axis_table(4)
     walls = []
     for weight in (plus, minus):
         wall = table.copy()
         wall[:32, :32] *= weight
         walls.append(np.concatenate([table, wall]))
-    return table.astype(np.float32), np.stack(walls).astype(np.float32)
-
-
-TABLE, WALL_TABLES = axis_tables()
+    return np.stack(walls).astype(np.float32)
+
+
+TOP = 7
+TABLE = axis_table(TOP)[0]
+WALL_TABLES = wall_tables()
 
 
 def dot(a, b):
@@ -100,21 +107,22 @@
     scale = inv * inv / (15.0 * n)
     grid = speed_grid()
     decay = tile4(-0.5 * inv)
-    columns = []
+    decays = []
     for u in (ux, uy, uz):
         w = grid - tile4(u)
-        g = jnp.exp(w * w * decay)
-        g1 = g * w
-        g2 = g1 * w
-        columns.append(jnp.concatenate([g, g1, g2, g2 * w], 1))
-    sums = dot(table, jnp.concatenate(columns, 0))
+        decays.append(jnp.exp(w * w * decay))
+    sums = dot(table, jnp.concatenate(decays, 0))
     factors = []
-    for axis, q in enumerate((qx, qy, qz)):
+    for axis, (u, q) in enumerate(((ux, qx), (uy, qy), (uz, qz))):
         kq = q * scale
+        base = 8 * TOP * axis
+        levels = [[sums[base + 8 * a : base + 8 * a + 8] for a in range(TOP)]]
+        for _ in range(3):
+            last = levels[-1]
+            levels.append([last[a + 1] - u * last[a] for a in range(len(last) - 1)])
         powers = []
         for power in range(4):
-            row = 32 * axis + 8 * power
-            t0, t1, t2, t3 = [sums[row : row + 8, CELLS * b : CELLS * (b + 1)] for b in range(4)]
+            t0, t1, t2, t3 = [level[power] for level in levels]
             powers.append((t0, kq * t1, t2 * inv, kq * (t3 * inv - 5.0 * t1)))
         factors.append(powers)
     xs, ys, zs = factors
@@ -219,24 +227,29 @@
     cxd = speed_x(p)
     cy, cz = lane_speeds(p, 8)
     d = lax.broadcasted_iota(jnp.int32, (8, HALF), 0)
-    common = jnp.where(d == 0, 1.0, 0.0)
-    common = jnp.where(d == 3, courant * jnp.maximum(cy, 0.0), common)
-    common = jnp.where(d == 4, courant * jnp.maximum(-cy, 0.0), common)
-    common = jnp.where(d == 5, courant * jnp.maximum(cz, 0.0), common)
-    common = jnp.where(d == 6, courant * jnp.maximum(-cz, 0.0), common)
+    yp, ym = courant * jnp.maximum(cy, 0.0), courant * jnp.maximum(-cy, 0.0)
+    zp, zm = courant * jnp.maximum(cz, 0.0), courant * jnp.maximum(-cz, 0.0)
     sign_a = jnp.where(odd == 0, 1.0, -1.0)
-    for w, sign, row in ((wa, sign_a, 1 + odd), (wb, -sign_a, 2 - odd)):
+    for w, sign in ((wa, sign_a), (wb, -sign_a)):
         cx = sign * cxd
-        multiplier = jnp.where(d == row, courant * cxd, common)
+        xp, xm = courant * jnp.maximum(cx, 0.0), courant * jnp.maximum(-cx, 0.0)
+        plus = jnp.where(d == 0, 1.0, jnp.where(d == 1, xp, jnp.where(d == 3, yp, jnp.where(d == 5, zp, 0.0))))
+        full = jnp.where(d == 2, xm, jnp.where(d == 4, ym, jnp.where(d == 6, zm, plus)))
         ypow = [1.0, cy, cy * cy, cy * cy * cy]
         zpow = [1.0, cz, cz * cz, cz * cz * cz]
         xpow = [1.0, cx, cx * cx, cx * cx * cx]
-        for k, terms in enumerate(MOMENTS):
+        phis = []
+        for terms in MOMENTS:
             phi = 0.0
             for ax, ay, az in terms:
                 phi = phi + xpow[ax] * (ypow[ay] * zpow[az])
-            w[8 * k : 8 * k + 8, :] = multiplier * phi
-        w[8 * NK : ROWS, :] = jnp.zeros((8, HALF), f32)
+            phis.append(phi)
+        gaps = jnp.where(d == 2, xp, jnp.where(d == 4, yp, jnp.where(d == 6, zp, 0.0)))
+        w[0:8, :] = plus * phis[0] + gaps * phis[3]
+        w[8:16, :] = plus * phis[1] + jnp.where(d == 2, phis[3], 0.0)
+        w[16:24, :] = plus * phis[2]
+        for k in range(4, NK):
+            w[8 * k - 8 : 8 * k, :] = full * phis[k]
     edge = jnp.where(jnp.logical_or(x == 0, x == 7), 1.0, 0.0)
     sub = lax.broadcasted_iota(jnp.int32, (8, CELLS), 0)
     temp = jnp.broadcast_to(temp_ref[pl.ds(face, 1), :], (8, CELLS))
@@ -259,13 +272,14 @@
         return carry
 
     lax.fori_loop(0, 16, step, 0, unroll=4)
-    flux = dot_t(jnp.full((8, HALF), 1.0, f32), fb[...]) * cxd
-    pre[8 * NK : ROWS, :] = flux * edge
+    flux = dot_t(jnp.full((8, HALF), 1.0, f32), fb[...]) * (cxd * edge)
     copy.wait()
-    in_rows = dot_t(wa[...], infl[...])
-    for k in range(NK):
-        pick = jnp.where(odd == 1, in_rows[8 * k + 2 : 8 * k + 3], in_rows[8 * k + 1 : 8 * k + 2])
-        pre[8 * k : 8 * k + 8, :] = jnp.where(sub == 7, jnp.broadcast_to(pick, (8, CELLS)), 0.0) * edge
+    in_rows = dot_t(wa[...], infl[...]) * (courant * cxd * edge)
+    for group in range(ROWS // 8):
+        value = jnp.where(sub == 7, spread(in_rows[8 * group : 8 * group + 1]), 0.0)
+        if group == 1:
+            value = jnp.where(sub == 6, spread(in_rows[10:11]), jnp.where(sub == 4, flux, value))
+        pre[8 * group : 8 * group + 8, :] = value
 
 
 def upwind_y(p, i):
@@ -283,27 +297,58 @@
     return value * centre + abs_x * plane + abs_y * neighbour_y + abs_z * neighbour_z
 
 
-def read_kernel(fa, fb, ha, hb, infl, cols, wa, wb, pre, ra, rb, keep, send):
-    x, p = here()
-    edge = jnp.where(jnp.logical_or(x == 0, x == 7), 1.0, 0.0)
+def read_b_kernel(fb, ha, wb, pre, rb, rows):
+    _, p = here()
     weights = transport_weights(speed_x(p), *lane_speeds(p, 16))
 
     def step(i, carry):
         at = pl.ds(pl.multiple_of(i * 16, 16), 16)
-        up = upwind_y(p, i)
+        rb[at, :] = transport_block(fb[at, :], fb[upwind_y(p, i), :], ha[at, :], weights)
+        return carry
+
+    lax.fori_loop(0, 16, step, 0, unroll=4)
+    rows[...] = pre[...] + dot_t(wb[...], rb[...])
+
+
+def read_a_kernel(fa, hb, infl, cols, wa, rows_b, ra, keep, send):
+    x, p = here()
+    inner = jnp.where(jnp.logical_or(x == 0, x == 7), 0.0, 1.0)
+    weights = transport_weights(speed_x(p), *lane_speeds(p, 16))
+
+    def step(i, carry):
+        at = pl.ds(pl.multiple_of(i * 16, 16), 16)
         c = cols[at, :]
         value = fa[at, :]
-        plane = hb[at, :] * (1.0 - edge) + infl[at, :] * c[:, 0:1] + c[:, 1:2] * value
-        ra[at, :] = transport_block(value, fa[up, :], plane, weights)
-        rb[at, :] = transport_block(fb[at, :], fb[up, :], ha[at, :], weights)
+        plane = hb[at, :] * inner + infl[at, :] * c[:, 0:1] + c[:, 1:2] * value
+        ra[at, :] = transport_block(value, fa[upwind_y(p, i), :], plane, weights)
         return carry
 
     lax.fori_loop(0, 16, step, 0, unroll=4)
-    rows = pre[...] + dot_t(wa[...], ra[...]) + dot_t(wb[...], rb[...])
+    rows = rows_b[...] + dot_t(wa[...], ra[...])
     north = p % 2 == 1
     top, bottom = rows[:HROWS], rows[HROWS:]
     keep[...] = jnp.where(north, bottom, top)
     send[...] = jnp.where(north, top, bottom)
+
+
+def unpack_rows(groups, sub):
+    first, second = groups[0], groups[1]
+    plain = [groups[0][:1], groups[1][:1], groups[2][:1], groups[1][2:3]] + [g[:1] for g in groups[3:]]
+    odd = jnp.logical_or(sub == 1, jnp.logical_or(sub == 3, sub == 5))
+    even = jnp.logical_or(sub == 2, jnp.logical_or(sub == 4, sub == 6))
+    products = [(1, 2, 3), (4, 7, 8), (7, 5, 9), (8, 9, 6)]
+
+    def less(plus, k):
+        ix, iy, iz = products[k]
+        change = jnp.where(sub == 2, spread(plain[ix]), jnp.where(sub == 4, spread(plain[iy]), spread(plain[iz])))
+        return plus - courant * change
+
+    out = []
+    for k in range(3):
+        out.append(jnp.where(even, less(pltpu.roll(groups[k], 1, 0), k), groups[k]))
+    rest = jnp.where(sub == 0, spread(second[2:3]), spread(second[6:7]))
+    out.append(jnp.where(odd, pltpu.roll(first, 7, 0), jnp.where(even, less(first, 3), rest)))
+    return out + list(groups[3:]), second[4:5]
 
 
 def cell_kernel(mine, other, wall, type_ref, table, send_a, send_b, own, state):
@@ -315,7 +360,8 @@
     north = p % 2 == 1
     a, b = mine[...], other[...]
     rows = jnp.concatenate([jnp.where(north, b, a), jnp.where(north, a, b)], 0)
-    m = [rows[8 * k : 8 * k + 8] for k in range(NK)]
+    sub = lax.broadcasted_iota(jnp.int32, (8, CELLS), 0)
+    m, leaving = unpack_rows([rows[8 * k : 8 * k + 8] for k in range(ROWS // 8)], sub)
     plain = [wall[8 * k : 8 * k + 8, :] for k in range(NK)]
     kind = jnp.broadcast_to(type_ref[pl.ds(face, 1), :], (8, CELLS))
     is_wall = jnp.where(kind == 0, edge, 0.0)
@@ -329,7 +375,7 @@
         return jnp.where(odd, v[1:2], v[2:3])
 
     entering = spread(first(plain[0])) * (1.0 / courant)
-    amp = is_wall * spread(rows[8 * NK : 8 * NK + 1]) / entering
+    amp = is_wall * spread(leaving) / entering
     inflow = [v[7:8] for v in m]
     m = [v + amp * wall[8 * (NK + k) : 8 * (NK + k) + 8, :] for k, v in enumerate(m)]
     params, rate = relax_params([spread(v[:1]) for v in m], table[...])
@@ -337,7 +383,6 @@
     inv = 1.0 / (1.0 + rate)
     m = [(v + rate * w) * inv for v, w in zip(m, s)]
     amp2 = is_wall * spread(second(m[0])) * (1.0 / courant) / entering
-    sub = lax.broadcasted_iota(jnp.int32, (8, CELLS), 0)
     lane = lax.broadcasted_iota(jnp.int32, (8, CELLS), 1)
     low, high = lane % 16 == 0, lane % 16 == 15
     for k in range(NK):
@@ -401,14 +446,14 @@
     return value * k[6] + (decay * pref) * (1.0 + (heat + heat_x) * (square + square_x))
 
 
-def own_kernel(ra, rb, state, wall_bulk, ca, cb, work):
+def own_kernel(ra, rb, state, wall_bulk, infl, cols, ca, cb, ghost, work):
     x, p = here()
     cxd = speed_x(p)
     sign_a = jnp.where(x % 2 == 0, 1.0, -1.0)
     cy, cz = lane_speeds(p, 16)
     st = state[...]
     rows = bulk_rows(
-        [st[k : k + 1] for k in range(8)], st[8:9], sign_a * cxd, -sign_a * cxd, [st[9:10] * (courant * cxd)]
+        [st[k : k + 1] for k in range(8)], st[8:9], sign_a * cxd, -sign_a * cxd, [st[9:10] * (courant * cxd), st[10:11]]
     )
     work[...] = to_columns(jnp.concatenate(rows, 0))
 
@@ -416,15 +461,43 @@
         at = pl.ds(pl.multiple_of(i * 16, 16), 16)
         k = columns(work[at, :], 0)
         part = shared_part(k, cy, cz)
-        ca[at, :] = relaxed(ra[at, :] + k[13] * wall_bulk[at, :], k, part, 0)
+        face = cols[at, :]
+        w = wall_bulk[at, :]
+        value = relaxed(ra[at, :] + k[13] * w, k, part, 0)
+        ca[at, :] = value
         cb[at, :] = relaxed(rb[at, :], k, part, 1)
+        ghost[at, :] = infl[at, :] * face[:, 0:1] + k[14] * w + face[:, 1:2] * value
         return carry
 
     lax.fori_loop(0, 16, step, 0, unroll=4)
 
 
+def halo_kernel(ha, from_a, wall_bulk, pb, work):
+    x, p = here()
+    cxd = speed_x(p)
+    cx = jnp.where(x % 2 == 0, -cxd, cxd)
+    cy, cz = lane_speeds(p, 16)
+    source = from_a[...]
+    rows = bulk_rows(
+        [source[NK + k : NK + k + 1] for k in range(8)],
+        source[NK + 8 : NK + 9],
+        cx,
+        cx,
+        [source[NK + 9 : NK + 10] * (courant * cxd)],
+    )
+    work[...] = to_columns(jnp.concatenate(rows, 0))
+
+    def step(i, carry):
+        at = pl.ds(pl.multiple_of(i * 16, 16), 16)
+        k = columns(work[at, :], 0)
+        pb[at, :] = relaxed(ha[at, :] + k[13] * wall_bulk[at, :], k, shared_part(k, cy, cz), 1)
+        return carry
+
+    lax.fori_loop(0, 16, step, 0, unroll=4)
+
+
 def final_kernel(
-    ca, cb, ha, hb, from_a, from_b, own, state, wall_bulk, infl, cols, table, out, fields, pa, pb, oa, ob, work, sems
+    ca, cb, pb, ghost, hb, from_a, from_b, own, state, table, out, fields, oa, ob, work, stage, sems
 ):
     x, p = here()
     odd = x % 2
@@ -434,64 +507,50 @@
     cy, cz = lane_speeds(p, 16)
     weights = transport_weights(cxd, cy, cz)
     edge = jnp.where(jnp.logical_or(x == 0, x == 7), 1.0, 0.0)
+    inner = 1.0 - edge
     ta, tb, st = from_a[...], from_b[...], state[...]
     m = [spread(own[k : k + 1, :] + ta[k : k + 1] + tb[k : k + 1]) for k in range(NK)]
     params, rate = relax_params(m, table[...])
-    wall_scale = courant * cxd
+    table8 = jnp.concatenate([v[:1] for v in params], 0)
+    for y in range(16):
+        stage[:, y, :] = table8[:, 16 * y : 16 * y + 16]
+    copies = [pltpu.make_async_copy(stage, fields, sems.at[8])]
+    copies[0].start()
     tb = jnp.where(edge > 0.0, st[:10], tb[NK : NK + 10])
-    ta = ta[NK : NK + 10]
-
-    def coefficients(source, extra=()):
-        return bulk_rows([source[k : k + 1] for k in range(8)], source[8:9], cx_a, cx_b, extra)
-
-    rows = coefficients(ta, [ta[9:10] * wall_scale])
-    rows += coefficients(tb, [jnp.zeros((1, CELLS), f32), st[10:11]])
+
+    rows = bulk_rows([tb[k : k + 1] for k in range(8)], tb[8:9], cx_a, cx_b)
     rows += bulk_rows([v[:1] for v in params], rate[:1], cx_a, cx_b)
     work[...] = to_columns(jnp.concatenate(rows, 0))
 
-    def first(i, carry):
-        at = pl.ds(pl.multiple_of(i * 16, 16), 16)
-        c = work[at, :]
-        k = cols[at, :]
-        w = wall_bulk[at, :]
-        ka, kb = columns(c, 0), columns(c, NCOL)
-        halo = relaxed(hb[at, :], kb, shared_part(kb, cy, cz), 0)
-        pa[at, :] = (1.0 - edge) * halo + infl[at, :] * k[:, 0:1] + kb[14] * w + k[:, 1:2] * ca[at, :]
-        pb[at, :] = relaxed(ha[at, :] + ka[13] * w, ka, shared_part(ka, cy, cz), 1)
-        return carry
-
-    lax.fori_loop(0, 16, first, 0, unroll=4)
-    copies = []
-    for chunk in range(4):
+    for chunk, (begin, end) in enumerate(((0, 5), (5, 10), (10, 14), (14, 16))):
 
         def second(i, carry):
             at = pl.ds(pl.multiple_of(i * 16, 16), 16)
             up = upwind_y(p, i)
-            k = columns(work[at, :], 2 * NCOL)
+            c = work[at, :]
+            kb, k = columns(c, 0), columns(c, NCOL)
             part = shared_part(k, cy, cz)
-            read = transport_block(ca[at, :], ca[up, :], pa[at, :], weights)
+            halo = relaxed(hb[at, :], kb, shared_part(kb, cy, cz), 0)
+            read = transport_block(ca[at, :], ca[up, :], inner * halo + ghost[at, :], weights)
             oa[at, :] = relaxed(read, k, part, 0)
             read = transport_block(cb[at, :], cb[up, :], pb[at, :], weights)
             ob[at, :] = relaxed(read, k, part, 1)
             return carry
 
-        lax.fori_loop(4 * chunk, 4 * chunk + 4, second, 0, unroll=4)
-        at = pl.ds(64 * chunk, 64)
+        lax.fori_loop(begin, end, second, 0, unroll=end - begin)
+        at = pl.ds(16 * begin, 16 * (end - begin))
         for half, source, start in ((0, oa, 1 - odd), (1, ob, odd)):
             copy = pltpu.make_async_copy(
                 source.at[at, :], out.at[at, pl.ds(half_start(start), HALF)], sems.at[2 * chunk + half]
             )
             copy.start()
             copies.append(copy)
-    table8 = jnp.concatenate([v[:1] for v in params], 0)
-    for y in range(16):
-        fields[:, y, :] = table8[:, 16 * y : 16 * y + 16]
     for copy in copies:
         copy.wait()
 
 
 VMEM = pl.BlockSpec(memory_space=pltpu.VMEM)
-ANY = pl.BlockSpec(memory_space=pl.ANY)
+ANY = pl.BlockSpec(memory_space=pltpu.HBM)
 PLANE = (CELLS, HALF)
 
 
@@ -546,10 +605,9 @@
         sems=1,
         loose_in=(0,),
     )
-    ra, rb, keep, send = call(
-        read_kernel,
-        [PLANE, PLANE, (HROWS, CELLS), (HROWS, CELLS)],
-        [fa, fb, ha, hb, infl, cols, wa, wb, pre],
+    rb, rows_b = call(read_b_kernel, [PLANE, (ROWS, CELLS)], [fb, ha, wb, pre])
+    ra, keep, send = call(
+        read_a_kernel, [PLANE, (HROWS, CELLS), (HROWS, CELLS)], [fa, hb, infl, cols, wa, rows_b]
     )
     part = keep + lax.ppermute(send, "core", SWAP)
     part = part + lax.ppermute(part, "ylo", SWAP)
@@ -567,14 +625,17 @@
         [part, other, wall, kind, table],
     )
     from_a, from_b = swap_planes(send_a, send_b)
-    ca, cb = call(own_kernel, [PLANE, PLANE], [ra, rb, state, wall_bulk], scratch=[(CELLS, 128)], cost=40_000_000)
+    ca, cb, ghost = call(
+        own_kernel, [PLANE] * 3, [ra, rb, state, wall_bulk, infl, cols], scratch=[(CELLS, 128)]
+    )
+    (pb,) = call(halo_kernel, [PLANE], [ga, from_a, wall_bulk], scratch=[(CELLS, 128)])
     out, fields = call(
         final_kernel,
         [(CELLS, 2 * HALF), (8, 16, 16)],
-        [ca, cb, ga, gb, from_a, from_b, own, state, wall_bulk, infl, cols, table],
-        scratch=[PLANE] * 4 + [(CELLS, 128)],
-        sems=8,
-        loose_out=(0,),
+        [ca, cb, pb, ghost, gb, from_a, from_b, own, state, table],
+        scratch=[PLANE] * 2 + [(CELLS, 128), (8, 16, 16)],
+        sems=9,
+        loose_out=(0, 1),
     )
     return out.reshape(1, 16, 16, 2 * HALF), fields[:, None]
 

time: 72.1 us -> 68.8 us (0.954)
  the two profiles are of different devices: /device:TPU:38 before, /device:TPU:6 now
where the time goes in v1:
time: 68.8 us; the launch traced here: 68.5 us
  starting transfers between devices  29.6 us (43%)
  waiting for transfers between devices  19.9 us (29%)
  Pallas kernels  12.7 us (18%)
  local copies, waits for them, and re-layouts  5.34 us (8%)
  between operations  0.94 us (1%)
    ppermute x3, starting transfers between devices, swap_planes(): b = lax.ppermute(b, 'space', PAIRS_B)  15.3 us
    pallas_call x8, Pallas kernels, call(): pl.pallas_call(kernel, out_shape=[jax.ShapeDtypeStruct(s, f32) for s in o...  12.7 us
    ppermute x3, starting transfers between devices, body(): part = part + lax.ppermute(part, 'z', pairs)  11.5 us
    ppermute x3, waiting for transfers between devices, swap_planes(): b = lax.ppermute(b, 'space', PAIRS_B)  8.2 us
    ppermute x3, waiting for transfers between devices, body(): part = part + lax.ppermute(part, 'z', pairs)  6.32 us
    unnamed x8, local copies, waits for them, and re-layouts  3.74 us
    ppermute x1, waiting for transfers between devices, body(): part = part + lax.ppermute(part, 'ylo', SWAP)  2.51 us
    ppermute x1, starting transfers between devices, body(): part = part + lax.ppermute(part, 'ylo', SWAP)  1.66 us
  transfers between devices with their start and end apart: 12, of which 9 were waited for; matrix products, arithmetic and copies ran while one was open for 2% of the time, Pallas kernels for 11%

profile of v1, /device:TPU:6, one launch (start us, length us, event | category | flops | bytes accessed | tf_op | source)
XLA Modules:
  0.0 68.5 jit_solution(15149438066971157920)
XLA Ops:
  0.6 0.0 copy-start.1
  0.6 1.2 %copy-done.1 = f32[1,16,16,1024]{3,2,1,0:T(8,128)S(1)} copy-done((f32[1,16,16,1024]{3,2,1,0:T(8,128)S(1)}, f32[1,16,16,1024]{3,2,1,0:T(8,128)}, u32[]{:S(2)}) %copy-start.1) | copy-done | bytes 1048600
  1.9 0.1 shard_map.77
  2.0 0.9 %collective-permute-start.1 = (f32[256,512]{1,0:T(8,128)S(1)}, f32[256,512]{1,0:T(8,128)S(1)}, u32[]{:S(2)}, u32[]{:S(2)}) collective-permute-start(f32[256,512]{1,0:T(8,128)S(1)} %get-tuple-element.27.fa), channel_id=1, source_target_pairs={{0,32},{32,0},{64,96},{96,64},{128,160},{160,128},{192,224},{224,1... | collective-permute-start | bytes 1572872 | tf_op jit(solution)/shard_map/ppermute | solution.py:590
  2.9 5.7 %collective-permute-start = (f32[256,512]{1,0:T(8,128)S(1)}, f32[256,512]{1,0:T(8,128)S(1)}, u32[]{:S(2)}, u32[]{:S(2)}) collective-permute-start(f32[256,512]{1,0:T(8,128)S(1)} %get-tuple-element.28.fb), channel_id=1, source_target_pairs={{32,64},{64,32},{96,128},{128,96},{160,192},{192,160},{33,65},{65,... | collective-permute-start | bytes 1572872 | tf_op jit(solution)/shard_map/ppermute | solution.py:589
  8.6 0.8 %reshape.21.temp_ref = f32[2,256]{1,0:T(2,128)S(1)} reshape(f32[2,16,16]{2,1,0:T(8,128)} %param.8) | data formatting | bytes 4096 | tf_op jit(solution)/shard_map/reshape | solution.py:598
  9.4 0.8 %reshape.22.type_ref = s32[2,256]{1,0:T(2,128)S(1)} reshape(s32[2,16,16]{2,1,0:T(8,128)} %param.9) | data formatting | bytes 4096 | tf_op jit(solution)/shard_map/reshape | solution.py:599
  10.2 0.0 copy-start
  10.2 1.6 %copy-done = f32[2,16,16,1024]{3,2,1,0:T(8,128)S(1)} copy-done((f32[2,16,16,1024]{3,2,1,0:T(8,128)S(1)}, f32[2,16,16,1024]{3,2,1,0:T(8,128)}, u32[]{:S(2)}) %copy-start) | copy-done | bytes 2097176
  11.8 0.0 copy-start.3
  11.8 0.9 %copy-done.3 = f32[2,192,96]{2,1,0:T(8,128)S(1)} copy-done((f32[2,192,96]{2,1,0:T(8,128)S(1)}, f32[2,192,96]{2,1,0:T(8,128)}, u32[]{:S(2)}) %copy-start.3) | copy-done | bytes 147480
  12.7 2.6 %shard_map.78 = (f32[256,512]{1,0:T(8,128)S(1)}, f32[96,512]{1,0:T(8,128)S(1)}, f32[96,512]{1,0:T(8,128)S(1)}, f32[96,256]{1,0:T(8,128)S(1)}, f32[208,256]{1,0:T...) custom-call(f32[2,256,1024]{2,1,0:T(8,128)S(1)} %bitcast.6, f32[256,512]{1,0:T(8,128)S(1)} %get-tuple-element.28.fb, ...), custom_call_target="tpu_custom_call" | custom-call | flops 1000000 | bytes 1048576 | tf_op jit(solution)/shard_map/pallas_call | solution.py:561
  15.3 0.0 copy-start.2
  15.4 0.4 collective-permute-done.1.ha
  15.7 0.9 %shard_map.79 = (f32[256,512]{1,0:T(8,128)S(1)}, f32[96,256]{1,0:T(8,128)S(1)}) custom-call(f32[256,512]{1,0:T(8,128)S(1)} %get-tuple-element.28.fb, f32[256,512]{1,0:T(8,128)S(1)} %collective-permute-done.1.ha, f32[96,512]{1,0:T(8,128)S(1)} %get-tuple-element.32.wb, f32[96,256]{1,0:T(8,128)S(1)} %get-tuple-element.33.pre), custom_call_target="tpu_custom_call" | custom-call | flops 1000000 | bytes 1048576 | tf_op jit(solution)/shard_map/pallas_call | solution.py:561
  16.6 5.2 %collective-permute-done.hb = f32[256,512]{1,0:T(8,128)S(1)} collective-permute-done((f32[256,512]{1,0:T(8,128)S(1)}, f32[256,512]{1,0:T(8,128)S(1)}, u32[]{:S(2)}, u32[]{:S(2)}) %collective-permute-start) | collective-permute-done | bytes 524320 | tf_op jit(solution)/shard_map/ppermute | solution.py:589
  21.8 1.1 %shard_map.80 = (f32[256,512]{1,0:T(8,128)S(1)}, f32[48,256]{1,0:T(8,128)S(1)}, f32[48,256]{1,0:T(8,128)S(1)}) custom-call(f32[256,512]{1,0:T(8,128)S(1)} %get-tuple-element.27.fa, f32[256,512]{1,0:T(8,128)S(1)} %collective-permute-done.hb, f32[256,512]{1,0:T(8,128)S(1)} %get-tuple-element.29.infl, f32[256,128]{1,0:T(8,128)S(1)} %get-tuple-element.30.cols, ...), custom_call_target="tpu_custom_call" | custom-call | flops 1000000 | bytes 1048576 | tf_op jit(solution)/shard_map/pallas_call | solution.py:561
  22.9 0.1 collective-permute-start.2
  23.0 1.2 %collective-permute-done.2 = f32[48,256]{1,0:T(8,128)S(1)} collective-permute-done((f32[48,256]{1,0:T(8,128)S(1)}, f32[48,256]{1,0:T(8,128)S(1)}, u32[]{:S(2)}, u32[]{:S(2)}) %collective-permute-start.2) | collective-permute-done | bytes 49184 | tf_op jit(solution)/shard_map/ppermute | solution.py:612
  24.2 1.7 %collective-permute-start.3 = (f32[48,256]{1,0:T(8,128)S(1)}, f32[48,256]{1,0:T(8,128)S(1)}, u32[]{:S(2)}, u32[]{:S(2)}) collective-permute-start(f32[48,256]{1,0:T(8,128)S(1)} %add.15), channel_id=1, source_target_pairs={{0,2},{2,0},{1,3},{3,1},{4,6},{6,4},{5,7},{7,5},{8,10},{10,8},{9,1... | collective-permute-start | bytes 147464 | tf_op jit(solution)/shard_map/ppermute | solution.py:613
  25.9 2.5 %collective-permute-done.3 = f32[48,256]{1,0:T(8,128)S(1)} collective-permute-done((f32[48,256]{1,0:T(8,128)S(1)}, f32[48,256]{1,0:T(8,128)S(1)}, u32[]{:S(2)}, u32[]{:S(2)}) %collective-permute-start.3) | collective-permute-done | bytes 49184 | tf_op jit(solution)/shard_map/ppermute | solution.py:613
  28.4 2.0 %collective-permute-start.4 = (f32[48,256]{1,0:T(8,128)S(1)}, f32[48,256]{1,0:T(8,128)S(1)}, u32[]{:S(2)}, u32[]{:S(2)}) collective-permute-start(f32[48,256]{1,0:T(8,128)S(1)} %add.16), channel_id=1, source_target_pairs={{0,4},{4,0},{8,12},{12,8},{16,20},{20,16},{24,28},{28,24},{1,5},{5... | collective-permute-start | bytes 147464 | tf_op jit(solution)/shard_map/ppermute | solution.py:619
  30.4 0.0 collective-permute-start.8
  30.4 2.2 %collective-permute-done.4 = f32[48,256]{1,0:T(8,128)S(1)} collective-permute-done((f32[48,256]{1,0:T(8,128)S(1)}, f32[48,256]{1,0:T(8,128)S(1)}, u32[]{:S(2)}, u32[]{:S(2)}) %collective-permute-start.4) | collective-permute-done | bytes 49184 | tf_op jit(solution)/shard_map/ppermute | solution.py:619
  32.6 5.8 %collective-permute-start.10 = (f32[256,512]{1,0:T(8,128)S(1)}, f32[256,512]{1,0:T(8,128)S(1)}, u32[]{:S(2)}, u32[]{:S(2)}) collective-permute-start(f32[256,512]{1,0:T(8,128)S(1)} %get-tuple-element.47.rb), channel_id=1, source_target_pairs={{32,64},{64,32},{96,128},{128,96},{160,192},{192,160},{33,65},{65,... | collective-permute-start | bytes 1572872 | tf_op jit(solution)/shard_map/ppermute | solution.py:589
  38.3 3.4 %collective-permute-start.5 = (f32[48,256]{1,0:T(8,128)S(1)}, f32[48,256]{1,0:T(8,128)S(1)}, u32[]{:S(2)}, u32[]{:S(2)}) collective-permute-start(f32[48,256]{1,0:T(8,128)S(1)} %add.17), channel_id=1, source_target_pairs={{0,8},{8,0},{4,12},{12,4},{16,24},{24,16},{20,28},{28,20},{1,9},{9... | collective-permute-start | bytes 147464 | tf_op jit(solution)/shard_map/ppermute | solution.py:619
  41.7 2.1 %collective-permute-done.5 = f32[48,256]{1,0:T(8,128)S(1)} collective-permute-done((f32[48,256]{1,0:T(8,128)S(1)}, f32[48,256]{1,0:T(8,128)S(1)}, u32[]{:S(2)}, u32[]{:S(2)}) %collective-permute-start.5) | collective-permute-done | bytes 49184 | tf_op jit(solution)/shard_map/ppermute | solution.py:619
  43.8 6.1 %collective-permute-start.6 = (f32[48,256]{1,0:T(8,128)S(1)}, f32[48,256]{1,0:T(8,128)S(1)}, u32[]{:S(2)}, u32[]{:S(2)}) collective-permute-start(f32[48,256]{1,0:T(8,128)S(1)} %add.18), channel_id=1, source_target_pairs={{0,24},{24,0},{4,28},{28,4},{8,16},{16,8},{12,20},{20,12},{1,25},{... | collective-permute-start | bytes 147464 | tf_op jit(solution)/shard_map/ppermute | solution.py:619
  49.9 2.1 %collective-permute-done.6 = f32[48,256]{1,0:T(8,128)S(1)} collective-permute-done((f32[48,256]{1,0:T(8,128)S(1)}, f32[48,256]{1,0:T(8,128)S(1)}, u32[]{:S(2)}, u32[]{:S(2)}) %collective-permute-start.6) | collective-permute-done | bytes 49184 | tf_op jit(solution)/shard_map/ppermute | solution.py:619
  52.0 0.1 collective-permute-start.7
  52.1 1.2 %collective-permute-done.7.other = f32[48,256]{1,0:T(8,128)S(1)} collective-permute-done((f32[48,256]{1,0:T(8,128)S(1)}, f32[48,256]{1,0:T(8,128)S(1)}, u32[]{:S(2)}, u32[]{:S(2)}) %collective-permute-start.7) | collective-permute-done | bytes 49184 | tf_op jit(solution)/shard_map/ppermute | solution.py:621
  53.3 0.0 copy-done.2
  53.3 1.8 %shard_map.81 = (f32[24,256]{1,0:T(8,128)S(1)}, f32[24,256]{1,0:T(8,128)S(1)}, f32[16,256]{1,0:T(8,128)S(1)}, f32[16,256]{1,0:T(8,128)S(1)}) custom-call(f32[48,256]{1,0:T(8,128)S(1)} %add.19.mine, f32[48,256]{1,0:T(8,128)S(1)} %collective-permute-done.7.other, f32[208,256]{1,0:T(8,128)S(1)} %get-tuple-element.39.wall, s32[2,256]{1,0:T(2,128)S(1)} %reshape.22.type_ref, ...), custom_call_target="tpu_custom_call" | custom-call | flops 1000000 | bytes 1048576 | tf_op jit(solution)/shard_map/pallas_call | solution.py:561
  55.1 0.1 collective-permute-start.9
  55.2 3.9 %collective-permute-start.11 = (f32[24,256]{1,0:T(8,128)S(1)}, f32[24,256]{1,0:T(8,128)S(1)}, u32[]{:S(2)}, u32[]{:S(2)}) collective-permute-start(f32[24,256]{1,0:T(8,128)S(1)} %get-tuple-element.48), channel_id=1, source_target_pairs={{32,64},{64,32},{96,128},{128,96},{160,192},{192,160},{33,65},{65,... | collective-permute-start | bytes 73736 | tf_op jit(solution)/shard_map/ppermute | solution.py:589
  59.1 1.4 %shard_map.82 = (f32[256,512]{1,0:T(8,128)S(1)}, f32[256,512]{1,0:T(8,128)S(1)}, f32[256,512]{1,0:T(8,128)S(1)}) custom-call(f32[256,512]{1,0:T(8,128)S(1)} %get-tuple-element.44.ra, f32[256,512]{1,0:T(8,128)S(1)} %get-tuple-element.47.rb, f32[16,256]{1,0:T(8,128)S(1)} %get-tuple-element.40.state, f32[256,512]{1,0:T(8,128)S(1)} %get-tuple-element.41.wall_bulk, ...), custom_call_target="tpu_custom_call" | custom-call | flops 1000000 | bytes 1048576 | tf_op jit(solution)/shard_map/pallas_call | solution.py:561
  60.4 0.0 collective-permute-done.9.from_a
  60.4 0.0 collective-permute-done.8.ha
  60.4 1.0 %shard_map.83.pb = f32[256,512]{1,0:T(8,128)S(1)} custom-call(f32[256,512]{1,0:T(8,128)S(1)} %collective-permute-done.8.ha, f32[24,256]{1,0:T(8,128)S(1)} %collective-permute-done.9.from_a, f32[256,512]{1,0:T(8,128)S(1)} %get-tuple-element.41.wall_bulk), custom_call_target="tpu_custom_call" | custom-call | flops 1000000 | bytes 1048576 | tf_op jit(solution)/shard_map/pallas_call | solution.py:561
  61.5 3.0 %collective-permute-done.11.from_b = f32[24,256]{1,0:T(8,128)S(1)} collective-permute-done((f32[24,256]{1,0:T(8,128)S(1)}, f32[24,256]{1,0:T(8,128)S(1)}, u32[]{:S(2)}, u32[]{:S(2)}) %collective-permute-start.11) | collective-permute-done | bytes 24608 | tf_op jit(solution)/shard_map/ppermute | solution.py:589
  64.5 0.0 collective-permute-done.10.hb
  64.5 3.8 %shard_map.84 = (f32[256,1024]{1,0:T(8,128)}, f32[8,16,16]{2,1,0:T(8,128)}) custom-call(f32[256,512]{1,0:T(8,128)S(1)} %get-tuple-element.42.ca, f32[256,512]{1,0:T(8,128)S(1)} %get-tuple-element.43.cb, f32[256,512]{1,0:T(8,128)S(1)} %shard_map.83.pb, f32[256,512]{1,0:T(8,128)S(1)} %get-tuple-element.46.ghost, f32[256,512]{1,0:T(8,128)S(1)} %collective-permute-done.10.hb, ...), custom_call_target="tpu_custom_call" | custom-call | flops 1000000 | bytes 1048576 | tf_op jit(solution)/shard_map/pallas_call | solution.py:561
  (5 shorter events, 0.0 us)
Async XLA Ops:
  0.6 1.2 %copy-start.1 = (f32[1,16,16,1024]{3,2,1,0:T(8,128)S(1)}, f32[1,16,16,1024]{3,2,1,0:T(8,128)}, u32[]{:S(2)}) copy-start(f32[1,16,16,1024]{3,2,1,0:T(8,128)} %param.6) | copy-start | bytes 3145732
  2.0 13.8 %collective-permute-start.1 = (f32[256,512]{1,0:T(8,128)S(1)}, f32[256,512]{1,0:T(8,128)S(1)}, u32[]{:S(2)}, u32[]{:S(2)}) collective-permute-start(f32[256,512]{1,0:T(8,128)S(1)} %get-tuple-element.27.fa), channel_id=1, source_target_pairs={{0,32},{32,0},{64,96},{96,64},{128,160},{160,128},{192,224},{224,1... | collective-permute-start | bytes 1572872 | tf_op jit(solution)/shard_map/ppermute | solution.py:590
  2.9 18.9 %collective-permute-start = (f32[256,512]{1,0:T(8,128)S(1)}, f32[256,512]{1,0:T(8,128)S(1)}, u32[]{:S(2)}, u32[]{:S(2)}) collective-permute-start(f32[256,512]{1,0:T(8,128)S(1)} %get-tuple-element.28.fb), channel_id=1, source_target_pairs={{32,64},{64,32},{96,128},{128,96},{160,192},{192,160},{33,65},{65,... | collective-permute-start | bytes 1572872 | tf_op jit(solution)/shard_map/ppermute | solution.py:589
  10.2 1.6 %copy-start = (f32[2,16,16,1024]{3,2,1,0:T(8,128)S(1)}, f32[2,16,16,1024]{3,2,1,0:T(8,128)}, u32[]{:S(2)}) copy-start(f32[2,16,16,1024]{3,2,1,0:T(8,128)} %param.7) | copy-start | bytes 6291460
  11.8 0.9 %copy-start.3 = (f32[2,192,96]{2,1,0:T(8,128)S(1)}, f32[2,192,96]{2,1,0:T(8,128)}, u32[]{:S(2)}) copy-start(f32[2,192,96]{2,1,0:T(8,128)} %constant.5.clone.tables) | copy-start | bytes 442372
  15.3 38.0 %copy-start.2 = (f32[168,96]{1,0:T(8,128)S(1)}, f32[168,96]{1,0:T(8,128)}, u32[]{:S(2)}) copy-start(f32[168,96]{1,0:T(8,128)} %constant.4.clone.table) | copy-start | bytes 193540
  22.9 1.3 %collective-permute-start.2 = (f32[48,256]{1,0:T(8,128)S(1)}, f32[48,256]{1,0:T(8,128)S(1)}, u32[]{:S(2)}, u32[]{:S(2)}) collective-permute-start(f32[48,256]{1,0:T(8,128)S(1)} %get-tuple-element.38), channel_id=1, source_target_pairs={{0,1},{1,0},{2,3},{3,2},{4,5},{5,4},{6,7},{7,6},{8,9},{9,8},{10,11... | collective-permute-start | bytes 147464 | tf_op jit(solution)/shard_map/ppermute | solution.py:612
  24.2 4.2 %collective-permute-start.3 = (f32[48,256]{1,0:T(8,128)S(1)}, f32[48,256]{1,0:T(8,128)S(1)}, u32[]{:S(2)}, u32[]{:S(2)}) collective-permute-start(f32[48,256]{1,0:T(8,128)S(1)} %add.15), channel_id=1, source_target_pairs={{0,2},{2,0},{1,3},{3,1},{4,6},{6,4},{5,7},{7,5},{8,10},{10,8},{9,1... | collective-permute-start | bytes 147464 | tf_op jit(solution)/shard_map/ppermute | solution.py:613
  28.4 4.2 %collective-permute-start.4 = (f32[48,256]{1,0:T(8,128)S(1)}, f32[48,256]{1,0:T(8,128)S(1)}, u32[]{:S(2)}, u32[]{:S(2)}) collective-permute-start(f32[48,256]{1,0:T(8,128)S(1)} %add.16), channel_id=1, source_target_pairs={{0,4},{4,0},{8,12},{12,8},{16,20},{20,16},{24,28},{28,24},{1,5},{5... | collective-permute-start | bytes 147464 | tf_op jit(solution)/shard_map/ppermute | solution.py:619
  30.4 30.1 %collective-permute-start.8 = (f32[256,512]{1,0:T(8,128)S(1)}, f32[256,512]{1,0:T(8,128)S(1)}, u32[]{:S(2)}, u32[]{:S(2)}) collective-permute-start(f32[256,512]{1,0:T(8,128)S(1)} %get-tuple-element.44.ra), channel_id=1, source_target_pairs={{0,32},{32,0},{64,96},{96,64},{128,160},{160,128},{192,224},{224,1... | collective-permute-start | bytes 1572872 | tf_op jit(solution)/shard_map/ppermute | solution.py:590
  32.6 31.9 %collective-permute-start.10 = (f32[256,512]{1,0:T(8,128)S(1)}, f32[256,512]{1,0:T(8,128)S(1)}, u32[]{:S(2)}, u32[]{:S(2)}) collective-permute-start(f32[256,512]{1,0:T(8,128)S(1)} %get-tuple-element.47.rb), channel_id=1, source_target_pairs={{32,64},{64,32},{96,128},{128,96},{160,192},{192,160},{33,65},{65,... | collective-permute-start | bytes 1572872 | tf_op jit(solution)/shard_map/ppermute | solution.py:589
  38.3 5.4 %collective-permute-start.5 = (f32[48,256]{1,0:T(8,128)S(1)}, f32[48,256]{1,0:T(8,128)S(1)}, u32[]{:S(2)}, u32[]{:S(2)}) collective-permute-start(f32[48,256]{1,0:T(8,128)S(1)} %add.17), channel_id=1, source_target_pairs={{0,8},{8,0},{4,12},{12,4},{16,24},{24,16},{20,28},{28,20},{1,9},{9... | collective-permute-start | bytes 147464 | tf_op jit(solution)/shard_map/ppermute | solution.py:619
  43.8 8.2 %collective-permute-start.6 = (f32[48,256]{1,0:T(8,128)S(1)}, f32[48,256]{1,0:T(8,128)S(1)}, u32[]{:S(2)}, u32[]{:S(2)}) collective-permute-start(f32[48,256]{1,0:T(8,128)S(1)} %add.18), channel_id=1, source_target_pairs={{0,24},{24,0},{4,28},{28,4},{8,16},{16,8},{12,20},{20,12},{1,25},{... | collective-permute-start | bytes 147464 | tf_op jit(solution)/shard_map/ppermute | solution.py:619
  52.0 1.3 %collective-permute-start.7 = (f32[48,256]{1,0:T(8,128)S(1)}, f32[48,256]{1,0:T(8,128)S(1)}, u32[]{:S(2)}, u32[]{:S(2)}) collective-permute-start(f32[48,256]{1,0:T(8,128)S(1)} %add.19.mine), channel_id=1, source_target_pairs={{0,1},{1,0},{2,3},{3,2},{4,5},{5,4},{6,7},{7,6},{8,9},{9,8},{10,11... | collective-permute-start | bytes 147464 | tf_op jit(solution)/shard_map/ppermute | solution.py:621
  55.1 5.3 %collective-permute-start.9 = (f32[24,256]{1,0:T(8,128)S(1)}, f32[24,256]{1,0:T(8,128)S(1)}, u32[]{:S(2)}, u32[]{:S(2)}) collective-permute-start(f32[24,256]{1,0:T(8,128)S(1)} %get-tuple-element.45), channel_id=1, source_target_pairs={{0,32},{32,0},{64,96},{96,64},{128,160},{160,128},{192,224},{224,1... | collective-permute-start | bytes 73736 | tf_op jit(solution)/shard_map/ppermute | solution.py:590
  55.2 9.3 %collective-permute-start.11 = (f32[24,256]{1,0:T(8,128)S(1)}, f32[24,256]{1,0:T(8,128)S(1)}, u32[]{:S(2)}, u32[]{:S(2)}) collective-permute-start(f32[24,256]{1,0:T(8,128)S(1)} %get-tuple-element.48), channel_id=1, source_target_pairs={{32,64},{64,32},{96,128},{128,96},{160,192},{192,160},{33,65},{65,... | collective-permute-start | bytes 73736 | tf_op jit(solution)/shard_map/ppermute | solution.py:589

commit v2 on v1

--- a/solution.py
+++ b/solution.py
@@ -63,7 +63,16 @@
 
 
 TOP = 7
-TABLE = axis_table(TOP)[0]
+
+
+def two_parts(table):
+    table = np.concatenate([table, np.zeros((-len(table) % 16, 96), np.float32)])
+    high = table.astype(jnp.bfloat16)
+    low = (table - high.astype(np.float32)).astype(jnp.bfloat16)
+    return np.concatenate([high, low])
+
+
+TABLE = two_parts(axis_table(TOP)[0])
 WALL_TABLES = wall_tables()
 
 
@@ -73,6 +82,20 @@
 
 def dot_t(a, b):
     return lax.dot_general(a, b, (((1,), (1,)), ((), ())), precision=HIGHEST, preferred_element_type=f32)
+
+
+def split(a):
+    high = a.astype(jnp.bfloat16)
+    return high, (a - high.astype(f32)).astype(jnp.bfloat16)
+
+
+def dot_parts(parts, b, side):
+    high, low = split(b)
+    rows = parts.shape[0] // 2
+    dims = (((1,), (side,)), ((), ()))
+    first = lax.dot_general(parts, high, dims, preferred_element_type=f32)
+    second = lax.dot_general(parts[:rows], low, dims, preferred_element_type=f32)
+    return first[:rows] + (first[rows:] + second)
 
 
 def tile4(a):
@@ -111,7 +134,7 @@
     for u in (ux, uy, uz):
         w = grid - tile4(u)
         decays.append(jnp.exp(w * w * decay))
-    sums = dot(table, jnp.concatenate(decays, 0))
+    sums = dot_parts(table, jnp.concatenate(decays, 0), 0)
     factors = []
     for axis, (u, q) in enumerate(((ux, qx), (uy, qy), (uz, qz))):
         kq = q * scale
@@ -218,7 +241,7 @@
     second.wait()
 
 
-def setup_kernel(inflow, fb, temp_ref, type_ref, tables, infl, wa, wb, pre, wall, wall_bulk, cols, sems):
+def setup_kernel(inflow, fb, temp_ref, type_ref, tables, infl, pa, pb, pre, wall, wall_bulk, cols, wa, wb, sems):
     x, p = here()
     odd = x % 2
     face = jnp.where(x >= 4, 1, 0)
@@ -272,6 +295,10 @@
         return carry
 
     lax.fori_loop(0, 16, step, 0, unroll=4)
+    for w, parts in ((wa, pa), (wb, pb)):
+        high, low = split(w[...])
+        parts[:ROWS, :] = high
+        parts[ROWS:, :] = low
     flux = dot_t(jnp.full((8, HALF), 1.0, f32), fb[...]) * (cxd * edge)
     copy.wait()
     in_rows = dot_t(wa[...], infl[...]) * (courant * cxd * edge)
@@ -307,7 +334,7 @@
         return carry
 
     lax.fori_loop(0, 16, step, 0, unroll=4)
-    rows[...] = pre[...] + dot_t(wb[...], rb[...])
+    rows[...] = pre[...] + dot_parts(wb[...], rb[...], 1)
 
 
 def read_a_kernel(fa, hb, infl, cols, wa, rows_b, ra, keep, send):
@@ -324,7 +351,7 @@
         return carry
 
     lax.fori_loop(0, 16, step, 0, unroll=4)
-    rows = rows_b[...] + dot_t(wa[...], ra[...])
+    rows = rows_b[...] + dot_parts(wa[...], ra[...], 1)
     north = p % 2 == 1
     top, bottom = rows[:HROWS], rows[HROWS:]
     keep[...] = jnp.where(north, bottom, top)
@@ -552,6 +579,7 @@
 VMEM = pl.BlockSpec(memory_space=pltpu.VMEM)
 ANY = pl.BlockSpec(memory_space=pltpu.HBM)
 PLANE = (CELLS, HALF)
+PARTS = (2 * ROWS, HALF)
 
 
 def call(kernel, outs, args, scratch=(), sems=0, loose_in=(), loose_out=(), cost=1_000_000, grant=16):
@@ -560,7 +588,7 @@
         scratches.append(pltpu.SemaphoreType.DMA((sems,)))
     return pl.pallas_call(
         kernel,
-        out_shape=[jax.ShapeDtypeStruct(s, f32) for s in outs],
+        out_shape=[jax.ShapeDtypeStruct(s, jnp.bfloat16 if s is PARTS else f32) for s in outs],
         in_specs=[ANY if k in loose_in else VMEM for k in range(len(args))],
         out_specs=[ANY if k in loose_out else VMEM for k in range(len(outs))],
         scratch_shapes=scratches,
@@ -600,8 +628,9 @@
     table = jnp.asarray(TABLE)
     infl, wa, wb, pre, wall, wall_bulk, cols = call(
         setup_kernel,
-        [PLANE, (ROWS, HALF), (ROWS, HALF), (ROWS, CELLS), (2 * NK * 8, CELLS), PLANE, (CELLS, 128)],
+        [PLANE, PARTS, PARTS, (ROWS, CELLS), (2 * NK * 8, CELLS), PLANE, (CELLS, 128)],
         [inflow.reshape(2, CELLS, 2 * HALF), fb, temp, kind, jnp.asarray(WALL_TABLES)],
+        scratch=[(ROWS, HALF)] * 2,
         sems=1,
         loose_in=(0,),
     )

time: 68.8 us -> 67.7 us (0.984)
  Pallas kernels: 12.7 us -> 11.5 us
    pallas_call x8, Pallas kernels: 12.7 us -> 11.5 us  [call(): pl.pallas_call(kernel, out_shape=[jax.ShapeDtypeStruct(s, jnp.bfloat16 if...]
where the time goes in v2:
time: 67.7 us; the launch traced here: 67.4 us
  starting transfers between devices  29.5 us (44%)
  waiting for transfers between devices  20.3 us (30%)
  Pallas kernels  11.5 us (17%)
  local copies, waits for them, and re-layouts  5.34 us (8%)
  between operations  0.77 us (1%)
    ppermute x3, starting transfers between devices, swap_planes(): b = lax.ppermute(b, 'space', PAIRS_B)  15.1 us
    pallas_call x8, Pallas kernels, call(): pl.pallas_call(kernel, out_shape=[jax.ShapeDtypeStruct(s, jnp.bfloat16 if...  11.5 us
    ppermute x3, starting transfers between devices, body(): part = part + lax.ppermute(part, 'z', pairs)  11.5 us
    ppermute x3, waiting for transfers between devices, swap_planes(): b = lax.ppermute(b, 'space', PAIRS_B)  8.69 us
    ppermute x3, waiting for transfers between devices, body(): part = part + lax.ppermute(part, 'z', pairs)  6.32 us
    unnamed x8, local copies, waits for them, and re-layouts  3.74 us
    ppermute x1, waiting for transfers between devices, body(): part = part + lax.ppermute(part, 'ylo', SWAP)  2.51 us
    ppermute x1, starting transfers between devices, body(): part = part + lax.ppermute(part, 'ylo', SWAP)  1.66 us
  transfers between devices with their start and end apart: 12, of which 9 were waited for; matrix products, arithmetic and copies ran while one was open for 2% of the time, Pallas kernels for 11%

profile of v2, /device:TPU:6, one launch (start us, length us, event | category | flops | bytes accessed | tf_op | source)
XLA Modules:
  0.0 67.4 jit_solution(11691681186293348205)
XLA Ops:
  0.6 0.0 copy-start.1
  0.6 1.2 %copy-done.1 = f32[1,16,16,1024]{3,2,1,0:T(8,128)S(1)} copy-done((f32[1,16,16,1024]{3,2,1,0:T(8,128)S(1)}, f32[1,16,16,1024]{3,2,1,0:T(8,128)}, u32[]{:S(2)}) %copy-start.1) | copy-done | bytes 1048600
  1.9 0.1 shard_map.77
  2.0 0.9 %collective-permute-start.1 = (f32[256,512]{1,0:T(8,128)S(1)}, f32[256,512]{1,0:T(8,128)S(1)}, u32[]{:S(2)}, u32[]{:S(2)}) collective-permute-start(f32[256,512]{1,0:T(8,128)S(1)} %get-tuple-element.27.fa), channel_id=1, source_target_pairs={{0,32},{32,0},{64,96},{96,64},{128,160},{160,128},{192,224},{224,1... | collective-permute-start | bytes 1572872 | tf_op jit(solution)/shard_map/ppermute | solution.py:618
  2.9 5.7 %collective-permute-start = (f32[256,512]{1,0:T(8,128)S(1)}, f32[256,512]{1,0:T(8,128)S(1)}, u32[]{:S(2)}, u32[]{:S(2)}) collective-permute-start(f32[256,512]{1,0:T(8,128)S(1)} %get-tuple-element.28.fb), channel_id=1, source_target_pairs={{32,64},{64,32},{96,128},{128,96},{160,192},{192,160},{33,65},{65,... | collective-permute-start | bytes 1572872 | tf_op jit(solution)/shard_map/ppermute | solution.py:617
  8.6 0.8 %reshape.21.temp_ref = f32[2,256]{1,0:T(2,128)S(1)} reshape(f32[2,16,16]{2,1,0:T(8,128)} %param.8) | data formatting | bytes 4096 | tf_op jit(solution)/shard_map/reshape | solution.py:626
  9.4 0.8 %reshape.22.type_ref = s32[2,256]{1,0:T(2,128)S(1)} reshape(s32[2,16,16]{2,1,0:T(8,128)} %param.9) | data formatting | bytes 4096 | tf_op jit(solution)/shard_map/reshape | solution.py:627
  10.2 0.0 copy-start
  10.2 1.6 %copy-done = f32[2,16,16,1024]{3,2,1,0:T(8,128)S(1)} copy-done((f32[2,16,16,1024]{3,2,1,0:T(8,128)S(1)}, f32[2,16,16,1024]{3,2,1,0:T(8,128)}, u32[]{:S(2)}) %copy-start) | copy-done | bytes 2097176
  11.8 0.0 copy-start.3
  11.8 0.9 %copy-done.3 = f32[2,192,96]{2,1,0:T(8,128)S(1)} copy-done((f32[2,192,96]{2,1,0:T(8,128)S(1)}, f32[2,192,96]{2,1,0:T(8,128)}, u32[]{:S(2)}) %copy-start.3) | copy-done | bytes 147480
  12.7 2.7 %shard_map.78 = (f32[256,512]{1,0:T(8,128)S(1)}, bf16[192,512]{1,0:T(8,128)(2,1)S(1)}, bf16[192,512]{1,0:T(8,128)(2,1)S(1)}, f32[96,256]{1,0:T(8,128)S(1)}, f32[...) custom-call(f32[2,256,1024]{2,1,0:T(8,128)S(1)} %bitcast.6, ...), custom_call_target="tpu_custom_call" | custom-call | flops 1000000 | bytes 1048576 | tf_op jit(solution)/shard_map/pallas_call | solution.py:589
  15.4 0.0 copy-start.2
  15.4 0.3 collective-permute-done.1.ha
  15.7 0.6 shard_map.79
  16.3 5.5 %collective-permute-done.hb = f32[256,512]{1,0:T(8,128)S(1)} collective-permute-done((f32[256,512]{1,0:T(8,128)S(1)}, f32[256,512]{1,0:T(8,128)S(1)}, u32[]{:S(2)}, u32[]{:S(2)}) %collective-permute-start) | collective-permute-done | bytes 524320 | tf_op jit(solution)/shard_map/ppermute | solution.py:617
  21.8 0.8 %shard_map.80 = (f32[256,512]{1,0:T(8,128)S(1)}, f32[48,256]{1,0:T(8,128)S(1)}, f32[48,256]{1,0:T(8,128)S(1)}) custom-call(f32[256,512]{1,0:T(8,128)S(1)} %get-tuple-element.27.fa, f32[256,512]{1,0:T(8,128)S(1)} %collective-permute-done.hb, f32[256,512]{1,0:T(8,128)S(1)} %get-tuple-element.29.infl, f32[256,128]{1,0:T(8,128)S(1)} %get-tuple-element.30.cols, ...), custom_call_target="tpu_custom_call" | custom-call | flops 1000000 | bytes 1048576 | tf_op jit(solution)/shard_map/pallas_call | solution.py:589
  22.6 0.1 collective-permute-start.2
  22.7 1.2 %collective-permute-done.2 = f32[48,256]{1,0:T(8,128)S(1)} collective-permute-done((f32[48,256]{1,0:T(8,128)S(1)}, f32[48,256]{1,0:T(8,128)S(1)}, u32[]{:S(2)}, u32[]{:S(2)}) %collective-permute-start.2) | collective-permute-done | bytes 49184 | tf_op jit(solution)/shard_map/ppermute | solution.py:641
  23.9 1.7 %collective-permute-start.3 = (f32[48,256]{1,0:T(8,128)S(1)}, f32[48,256]{1,0:T(8,128)S(1)}, u32[]{:S(2)}, u32[]{:S(2)}) collective-permute-start(f32[48,256]{1,0:T(8,128)S(1)} %add.15), channel_id=1, source_target_pairs={{0,2},{2,0},{1,3},{3,1},{4,6},{6,4},{5,7},{7,5},{8,10},{10,8},{9,1... | collective-permute-start | bytes 147464 | tf_op jit(solution)/shard_map/ppermute | solution.py:642
  25.6 2.5 %collective-permute-done.3 = f32[48,256]{1,0:T(8,128)S(1)} collective-permute-done((f32[48,256]{1,0:T(8,128)S(1)}, f32[48,256]{1,0:T(8,128)S(1)}, u32[]{:S(2)}, u32[]{:S(2)}) %collective-permute-start.3) | collective-permute-done | bytes 49184 | tf_op jit(solution)/shard_map/ppermute | solution.py:642
  28.1 2.0 %collective-permute-start.4 = (f32[48,256]{1,0:T(8,128)S(1)}, f32[48,256]{1,0:T(8,128)S(1)}, u32[]{:S(2)}, u32[]{:S(2)}) collective-permute-start(f32[48,256]{1,0:T(8,128)S(1)} %add.16), channel_id=1, source_target_pairs={{0,4},{4,0},{8,12},{12,8},{16,20},{20,16},{24,28},{28,24},{1,5},{5... | collective-permute-start | bytes 147464 | tf_op jit(solution)/shard_map/ppermute | solution.py:648
  30.1 0.0 collective-permute-start.8
  30.1 2.2 %collective-permute-done.4 = f32[48,256]{1,0:T(8,128)S(1)} collective-permute-done((f32[48,256]{1,0:T(8,128)S(1)}, f32[48,256]{1,0:T(8,128)S(1)}, u32[]{:S(2)}, u32[]{:S(2)}) %collective-permute-start.4) | collective-permute-done | bytes 49184 | tf_op jit(solution)/shard_map/ppermute | solution.py:648
  32.3 5.8 %collective-permute-start.10 = (f32[256,512]{1,0:T(8,128)S(1)}, f32[256,512]{1,0:T(8,128)S(1)}, u32[]{:S(2)}, u32[]{:S(2)}) collective-permute-start(f32[256,512]{1,0:T(8,128)S(1)} %get-tuple-element.47.rb), channel_id=1, source_target_pairs={{32,64},{64,32},{96,128},{128,96},{160,192},{192,160},{33,65},{65,... | collective-permute-start | bytes 1572872 | tf_op jit(solution)/shard_map/ppermute | solution.py:617
  38.1 3.4 %collective-permute-start.5 = (f32[48,256]{1,0:T(8,128)S(1)}, f32[48,256]{1,0:T(8,128)S(1)}, u32[]{:S(2)}, u32[]{:S(2)}) collective-permute-start(f32[48,256]{1,0:T(8,128)S(1)} %add.17), channel_id=1, source_target_pairs={{0,8},{8,0},{4,12},{12,4},{16,24},{24,16},{20,28},{28,20},{1,9},{9... | collective-permute-start | bytes 147464 | tf_op jit(solution)/shard_map/ppermute | solution.py:648
  41.4 2.1 %collective-permute-done.5 = f32[48,256]{1,0:T(8,128)S(1)} collective-permute-done((f32[48,256]{1,0:T(8,128)S(1)}, f32[48,256]{1,0:T(8,128)S(1)}, u32[]{:S(2)}, u32[]{:S(2)}) %collective-permute-start.5) | collective-permute-done | bytes 49184 | tf_op jit(solution)/shard_map/ppermute | solution.py:648
  43.5 6.1 %collective-permute-start.6 = (f32[48,256]{1,0:T(8,128)S(1)}, f32[48,256]{1,0:T(8,128)S(1)}, u32[]{:S(2)}, u32[]{:S(2)}) collective-permute-start(f32[48,256]{1,0:T(8,128)S(1)} %add.18), channel_id=1, source_target_pairs={{0,24},{24,0},{4,28},{28,4},{8,16},{16,8},{12,20},{20,12},{1,25},{... | collective-permute-start | bytes 147464 | tf_op jit(solution)/shard_map/ppermute | solution.py:648
  49.6 2.1 %collective-permute-done.6 = f32[48,256]{1,0:T(8,128)S(1)} collective-permute-done((f32[48,256]{1,0:T(8,128)S(1)}, f32[48,256]{1,0:T(8,128)S(1)}, u32[]{:S(2)}, u32[]{:S(2)}) %collective-permute-start.6) | collective-permute-done | bytes 49184 | tf_op jit(solution)/shard_map/ppermute | solution.py:648
  51.7 0.1 collective-permute-start.7
  51.8 1.2 %collective-permute-done.7.other = f32[48,256]{1,0:T(8,128)S(1)} collective-permute-done((f32[48,256]{1,0:T(8,128)S(1)}, f32[48,256]{1,0:T(8,128)S(1)}, u32[]{:S(2)}, u32[]{:S(2)}) %collective-permute-start.7) | collective-permute-done | bytes 49184 | tf_op jit(solution)/shard_map/ppermute | solution.py:650
  53.0 0.0 copy-done.2
  53.0 1.4 %shard_map.81 = (f32[24,256]{1,0:T(8,128)S(1)}, f32[24,256]{1,0:T(8,128)S(1)}, f32[16,256]{1,0:T(8,128)S(1)}, f32[16,256]{1,0:T(8,128)S(1)}) custom-call(f32[48,256]{1,0:T(8,128)S(1)} %add.19.mine, f32[48,256]{1,0:T(8,128)S(1)} %collective-permute-done.7.other, f32[208,256]{1,0:T(8,128)S(1)} %get-tuple-element.39.wall, s32[2,256]{1,0:T(2,128)S(1)} %reshape.22.type_ref, ...), custom_call_target="tpu_custom_call" | custom-call | flops 1000000 | bytes 1048576 | tf_op jit(solution)/shard_map/pallas_call | solution.py:589
  54.5 0.1 collective-permute-start.9
  54.6 3.7 %collective-permute-start.11 = (f32[24,256]{1,0:T(8,128)S(1)}, f32[24,256]{1,0:T(8,128)S(1)}, u32[]{:S(2)}, u32[]{:S(2)}) collective-permute-start(f32[24,256]{1,0:T(8,128)S(1)} %get-tuple-element.48), channel_id=1, source_target_pairs={{32,64},{64,32},{96,128},{128,96},{160,192},{192,160},{33,65},{65,... | collective-permute-start | bytes 73736 | tf_op jit(solution)/shard_map/ppermute | solution.py:617
  58.3 1.4 %shard_map.82 = (f32[256,512]{1,0:T(8,128)S(1)}, f32[256,512]{1,0:T(8,128)S(1)}, f32[256,512]{1,0:T(8,128)S(1)}) custom-call(f32[256,512]{1,0:T(8,128)S(1)} %get-tuple-element.44.ra, f32[256,512]{1,0:T(8,128)S(1)} %get-tuple-element.47.rb, f32[16,256]{1,0:T(8,128)S(1)} %get-tuple-element.40.state, f32[256,512]{1,0:T(8,128)S(1)} %get-tuple-element.41.wall_bulk, ...), custom_call_target="tpu_custom_call" | custom-call | flops 1000000 | bytes 1048576 | tf_op jit(solution)/shard_map/pallas_call | solution.py:589
  59.6 0.0 collective-permute-done.9.from_a
  59.6 0.0 collective-permute-done.8.ha
  59.6 1.0 %shard_map.83.pb = f32[256,512]{1,0:T(8,128)S(1)} custom-call(f32[256,512]{1,0:T(8,128)S(1)} %collective-permute-done.8.ha, f32[24,256]{1,0:T(8,128)S(1)} %collective-permute-done.9.from_a, f32[256,512]{1,0:T(8,128)S(1)} %get-tuple-element.41.wall_bulk), custom_call_target="tpu_custom_call" | custom-call | flops 1000000 | bytes 1048576 | tf_op jit(solution)/shard_map/pallas_call | solution.py:589
  60.7 3.2 %collective-permute-done.11.from_b = f32[24,256]{1,0:T(8,128)S(1)} collective-permute-done((f32[24,256]{1,0:T(8,128)S(1)}, f32[24,256]{1,0:T(8,128)S(1)}, u32[]{:S(2)}, u32[]{:S(2)}) %collective-permute-start.11) | collective-permute-done | bytes 24608 | tf_op jit(solution)/shard_map/ppermute | solution.py:617
  63.9 0.0 collective-permute-done.10.hb
  63.9 3.5 %shard_map.84 = (f32[256,1024]{1,0:T(8,128)}, f32[8,16,16]{2,1,0:T(8,128)}) custom-call(f32[256,512]{1,0:T(8,128)S(1)} %get-tuple-element.42.ca, f32[256,512]{1,0:T(8,128)S(1)} %get-tuple-element.43.cb, f32[256,512]{1,0:T(8,128)S(1)} %shard_map.83.pb, f32[256,512]{1,0:T(8,128)S(1)} %get-tuple-element.46.ghost, f32[256,512]{1,0:T(8,128)S(1)} %collective-permute-done.10.hb, ...), custom_call_target="tpu_custom_call" | custom-call | flops 1000000 | bytes 1048576 | tf_op jit(solution)/shard_map/pallas_call | solution.py:589
  (5 shorter events, 0.0 us)
Async XLA Ops:
  0.6 1.2 %copy-start.1 = (f32[1,16,16,1024]{3,2,1,0:T(8,128)S(1)}, f32[1,16,16,1024]{3,2,1,0:T(8,128)}, u32[]{:S(2)}) copy-start(f32[1,16,16,1024]{3,2,1,0:T(8,128)} %param.6) | copy-start | bytes 3145732
  2.0 13.8 %collective-permute-start.1 = (f32[256,512]{1,0:T(8,128)S(1)}, f32[256,512]{1,0:T(8,128)S(1)}, u32[]{:S(2)}, u32[]{:S(2)}) collective-permute-start(f32[256,512]{1,0:T(8,128)S(1)} %get-tuple-element.27.fa), channel_id=1, source_target_pairs={{0,32},{32,0},{64,96},{96,64},{128,160},{160,128},{192,224},{224,1... | collective-permute-start | bytes 1572872 | tf_op jit(solution)/shard_map/ppermute | solution.py:618
  2.9 18.9 %collective-permute-start = (f32[256,512]{1,0:T(8,128)S(1)}, f32[256,512]{1,0:T(8,128)S(1)}, u32[]{:S(2)}, u32[]{:S(2)}) collective-permute-start(f32[256,512]{1,0:T(8,128)S(1)} %get-tuple-element.28.fb), channel_id=1, source_target_pairs={{32,64},{64,32},{96,128},{128,96},{160,192},{192,160},{33,65},{65,... | collective-permute-start | bytes 1572872 | tf_op jit(solution)/shard_map/ppermute | solution.py:617
  10.2 1.6 %copy-start = (f32[2,16,16,1024]{3,2,1,0:T(8,128)S(1)}, f32[2,16,16,1024]{3,2,1,0:T(8,128)}, u32[]{:S(2)}) copy-start(f32[2,16,16,1024]{3,2,1,0:T(8,128)} %param.7) | copy-start | bytes 6291460
  11.8 0.9 %copy-start.3 = (f32[2,192,96]{2,1,0:T(8,128)S(1)}, f32[2,192,96]{2,1,0:T(8,128)}, u32[]{:S(2)}) copy-start(f32[2,192,96]{2,1,0:T(8,128)} %constant.5.clone.tables) | copy-start | bytes 442372
  15.4 37.6 %copy-start.2 = (bf16[352,96]{1,0:T(8,128)(2,1)S(1)}, bf16[352,96]{1,0:T(8,128)(2,1)}, u32[]{:S(2)}) copy-start(bf16[352,96]{1,0:T(8,128)(2,1)} %constant.4.clone.table) | copy-start | bytes 202756
  22.6 1.3 %collective-permute-start.2 = (f32[48,256]{1,0:T(8,128)S(1)}, f32[48,256]{1,0:T(8,128)S(1)}, u32[]{:S(2)}, u32[]{:S(2)}) collective-permute-start(f32[48,256]{1,0:T(8,128)S(1)} %get-tuple-element.38), channel_id=1, source_target_pairs={{0,1},{1,0},{2,3},{3,2},{4,5},{5,4},{6,7},{7,6},{8,9},{9,8},{10,11... | collective-permute-start | bytes 147464 | tf_op jit(solution)/shard_map/ppermute | solution.py:641
  23.9 4.2 %collective-permute-start.3 = (f32[48,256]{1,0:T(8,128)S(1)}, f32[48,256]{1,0:T(8,128)S(1)}, u32[]{:S(2)}, u32[]{:S(2)}) collective-permute-start(f32[48,256]{1,0:T(8,128)S(1)} %add.15), channel_id=1, source_target_pairs={{0,2},{2,0},{1,3},{3,1},{4,6},{6,4},{5,7},{7,5},{8,10},{10,8},{9,1... | collective-permute-start | bytes 147464 | tf_op jit(solution)/shard_map/ppermute | solution.py:642
  28.1 4.2 %collective-permute-start.4 = (f32[48,256]{1,0:T(8,128)S(1)}, f32[48,256]{1,0:T(8,128)S(1)}, u32[]{:S(2)}, u32[]{:S(2)}) collective-permute-start(f32[48,256]{1,0:T(8,128)S(1)} %add.16), channel_id=1, source_target_pairs={{0,4},{4,0},{8,12},{12,8},{16,20},{20,16},{24,28},{28,24},{1,5},{5... | collective-permute-start | bytes 147464 | tf_op jit(solution)/shard_map/ppermute | solution.py:648
  30.1 29.5 %collective-permute-start.8 = (f32[256,512]{1,0:T(8,128)S(1)}, f32[256,512]{1,0:T(8,128)S(1)}, u32[]{:S(2)}, u32[]{:S(2)}) collective-permute-start(f32[256,512]{1,0:T(8,128)S(1)} %get-tuple-element.44.ra), channel_id=1, source_target_pairs={{0,32},{32,0},{64,96},{96,64},{128,160},{160,128},{192,224},{224,1... | collective-permute-start | bytes 1572872 | tf_op jit(solution)/shard_map/ppermute | solution.py:618
  32.3 31.6 %collective-permute-start.10 = (f32[256,512]{1,0:T(8,128)S(1)}, f32[256,512]{1,0:T(8,128)S(1)}, u32[]{:S(2)}, u32[]{:S(2)}) collective-permute-start(f32[256,512]{1,0:T(8,128)S(1)} %get-tuple-element.47.rb), channel_id=1, source_target_pairs={{32,64},{64,32},{96,128},{128,96},{160,192},{192,160},{33,65},{65,... | collective-permute-start | bytes 1572872 | tf_op jit(solution)/shard_map/ppermute | solution.py:617
  38.1 5.4 %collective-permute-start.5 = (f32[48,256]{1,0:T(8,128)S(1)}, f32[48,256]{1,0:T(8,128)S(1)}, u32[]{:S(2)}, u32[]{:S(2)}) collective-permute-start(f32[48,256]{1,0:T(8,128)S(1)} %add.17), channel_id=1, source_target_pairs={{0,8},{8,0},{4,12},{12,4},{16,24},{24,16},{20,28},{28,20},{1,9},{9... | collective-permute-start | bytes 147464 | tf_op jit(solution)/shard_map/ppermute | solution.py:648
  43.5 8.2 %collective-permute-start.6 = (f32[48,256]{1,0:T(8,128)S(1)}, f32[48,256]{1,0:T(8,128)S(1)}, u32[]{:S(2)}, u32[]{:S(2)}) collective-permute-start(f32[48,256]{1,0:T(8,128)S(1)} %add.18), channel_id=1, source_target_pairs={{0,24},{24,0},{4,28},{28,4},{8,16},{16,8},{12,20},{20,12},{1,25},{... | collective-permute-start | bytes 147464 | tf_op jit(solution)/shard_map/ppermute | solution.py:648
  51.7 1.3 %collective-permute-start.7 = (f32[48,256]{1,0:T(8,128)S(1)}, f32[48,256]{1,0:T(8,128)S(1)}, u32[]{:S(2)}, u32[]{:S(2)}) collective-permute-start(f32[48,256]{1,0:T(8,128)S(1)} %add.19.mine), channel_id=1, source_target_pairs={{0,1},{1,0},{2,3},{3,2},{4,5},{5,4},{6,7},{7,6},{8,9},{9,8},{10,11... | collective-permute-start | bytes 147464 | tf_op jit(solution)/shard_map/ppermute | solution.py:650
  54.5 5.2 %collective-permute-start.9 = (f32[24,256]{1,0:T(8,128)S(1)}, f32[24,256]{1,0:T(8,128)S(1)}, u32[]{:S(2)}, u32[]{:S(2)}) collective-permute-start(f32[24,256]{1,0:T(8,128)S(1)} %get-tuple-element.45), channel_id=1, source_target_pairs={{0,32},{32,0},{64,96},{96,64},{128,160},{160,128},{192,224},{224,1... | collective-permute-start | bytes 73736 | tf_op jit(solution)/shard_map/ppermute | solution.py:618
  54.6 9.3 %collective-permute-start.11 = (f32[24,256]{1,0:T(8,128)S(1)}, f32[24,256]{1,0:T(8,128)S(1)}, u32[]{:S(2)}, u32[]{:S(2)}) collective-permute-start(f32[24,256]{1,0:T(8,128)S(1)} %get-tuple-element.48), channel_id=1, source_target_pairs={{32,64},{64,32},{96,128},{128,96},{160,192},{192,160},{33,65},{65,... | collective-permute-start | bytes 73736 | tf_op jit(solution)/shard_map/ppermute | solution.py:617

commit v3 on v2

--- a/solution.py
+++ b/solution.py
@@ -62,7 +62,7 @@
     return np.stack(walls).astype(np.float32)
 
 
-TOP = 7
+TOP = 5
 
 
 def two_parts(table):
@@ -94,8 +94,8 @@
     rows = parts.shape[0] // 2
     dims = (((1,), (side,)), ((), ()))
     first = lax.dot_general(parts, high, dims, preferred_element_type=f32)
-    second = lax.dot_general(parts[:rows], low, dims, preferred_element_type=f32)
-    return first[:rows] + (first[rows:] + second)
+    second = lax.dot_general(parts, low, dims, preferred_element_type=f32)
+    return first[:rows] + (first[rows:] + second[:rows] + second[rows:])
 
 
 def tile4(a):
@@ -130,22 +130,24 @@
     scale = inv * inv / (15.0 * n)
     grid = speed_grid()
     decay = tile4(-0.5 * inv)
-    decays = []
+    columns = []
     for u in (ux, uy, uz):
         w = grid - tile4(u)
-        decays.append(jnp.exp(w * w * decay))
-    sums = dot_parts(table, jnp.concatenate(decays, 0), 0)
+        square = w * w
+        g = jnp.exp(square * decay)
+        columns.append(jnp.concatenate([g, g * square], 1))
+    sums = dot_parts(table, jnp.concatenate(columns, 0), 0)
     factors = []
     for axis, (u, q) in enumerate(((ux, qx), (uy, qy), (uz, qz))):
         kq = q * scale
-        base = 8 * TOP * axis
-        levels = [[sums[base + 8 * a : base + 8 * a + 8] for a in range(TOP)]]
-        for _ in range(3):
-            last = levels[-1]
-            levels.append([last[a + 1] - u * last[a] for a in range(len(last) - 1)])
+        starts = [8 * (TOP * axis + power) for power in range(TOP)]
+        even0 = [sums[row : row + 8, :CELLS] for row in starts]
+        even2 = [sums[row : row + 8, CELLS:] for row in starts]
         powers = []
         for power in range(4):
-            t0, t1, t2, t3 = [level[power] for level in levels]
+            t0, t2 = even0[power], even2[power]
+            t1 = even0[power + 1] - u * t0
+            t3 = even2[power + 1] - u * t2
             powers.append((t0, kq * t1, t2 * inv, kq * (t3 * inv - 5.0 * t1)))
         factors.append(powers)
     xs, ys, zs = factors

time: 67.7 us -> 67.9 us (level)
  no operation moved by 1% of the time
where the time goes in v3:
time: 67.9 us; the launch traced here: 67.5 us
  starting transfers between devices  29.5 us (43%)
  waiting for transfers between devices  20.3 us (30%)
  Pallas kernels  11.6 us (17%)
  local copies, waits for them, and re-layouts  5.34 us (8%)
  between operations  0.78 us (1%)
    ppermute x3, starting transfers between devices, swap_planes(): b = lax.ppermute(b, 'space', PAIRS_B)  15.1 us
    pallas_call x8, Pallas kernels, call(): pl.pallas_call(kernel, out_shape=[jax.ShapeDtypeStruct(s, jnp.bfloat16 if...  11.6 us
    ppermute x3, starting transfers between devices, body(): part = part + lax.ppermute(part, 'z', pairs)  11.5 us
    ppermute x3, waiting for transfers between devices, swap_planes(): b = lax.ppermute(b, 'space', PAIRS_B)  8.68 us
    ppermute x3, waiting for transfers between devices, body(): part = part + lax.ppermute(part, 'z', pairs)  6.32 us
    unnamed x8, local copies, waits for them, and re-layouts  3.74 us
    ppermute x1, waiting for transfers between devices, body(): part = part + lax.ppermute(part, 'ylo', SWAP)  2.51 us
    ppermute x1, starting transfers between devices, body(): part = part + lax.ppermute(part, 'ylo', SWAP)  1.66 us
  transfers between devices with their start and end apart: 12, of which 9 were waited for; matrix products, arithmetic and copies ran while one was open for 2% of the time, Pallas kernels for 11%

profile of v3, /device:TPU:6, one launch (start us, length us, event | category | flops | bytes accessed | tf_op | source)
XLA Modules:
  0.0 67.5 jit_solution(8694478411311770246)
XLA Ops:
  0.6 0.0 copy-start.1
  0.6 1.2 %copy-done.1 = f32[1,16,16,1024]{3,2,1,0:T(8,128)S(1)} copy-done((f32[1,16,16,1024]{3,2,1,0:T(8,128)S(1)}, f32[1,16,16,1024]{3,2,1,0:T(8,128)}, u32[]{:S(2)}) %copy-start.1) | copy-done | bytes 1048600
  1.9 0.1 shard_map.77
  2.0 0.9 %collective-permute-start.1 = (f32[256,512]{1,0:T(8,128)S(1)}, f32[256,512]{1,0:T(8,128)S(1)}, u32[]{:S(2)}, u32[]{:S(2)}) collective-permute-start(f32[256,512]{1,0:T(8,128)S(1)} %get-tuple-element.27.fa), channel_id=1, source_target_pairs={{0,32},{32,0},{64,96},{96,64},{128,160},{160,128},{192,224},{224,1... | collective-permute-start | bytes 1572872 | tf_op jit(solution)/shard_map/ppermute | solution.py:620
  2.9 5.7 %collective-permute-start = (f32[256,512]{1,0:T(8,128)S(1)}, f32[256,512]{1,0:T(8,128)S(1)}, u32[]{:S(2)}, u32[]{:S(2)}) collective-permute-start(f32[256,512]{1,0:T(8,128)S(1)} %get-tuple-element.28.fb), channel_id=1, source_target_pairs={{32,64},{64,32},{96,128},{128,96},{160,192},{192,160},{33,65},{65,... | collective-permute-start | bytes 1572872 | tf_op jit(solution)/shard_map/ppermute | solution.py:619
  8.6 0.8 %reshape.21.temp_ref = f32[2,256]{1,0:T(2,128)S(1)} reshape(f32[2,16,16]{2,1,0:T(8,128)} %param.8) | data formatting | bytes 4096 | tf_op jit(solution)/shard_map/reshape | solution.py:628
  9.4 0.8 %reshape.22.type_ref = s32[2,256]{1,0:T(2,128)S(1)} reshape(s32[2,16,16]{2,1,0:T(8,128)} %param.9) | data formatting | bytes 4096 | tf_op jit(solution)/shard_map/reshape | solution.py:629
  10.2 0.0 copy-start
  10.2 1.6 %copy-done = f32[2,16,16,1024]{3,2,1,0:T(8,128)S(1)} copy-done((f32[2,16,16,1024]{3,2,1,0:T(8,128)S(1)}, f32[2,16,16,1024]{3,2,1,0:T(8,128)}, u32[]{:S(2)}) %copy-start) | copy-done | bytes 2097176
  11.8 0.0 copy-start.3
  11.8 0.9 %copy-done.3 = f32[2,192,96]{2,1,0:T(8,128)S(1)} copy-done((f32[2,192,96]{2,1,0:T(8,128)S(1)}, f32[2,192,96]{2,1,0:T(8,128)}, u32[]{:S(2)}) %copy-start.3) | copy-done | bytes 147480
  12.7 2.7 %shard_map.78 = (f32[256,512]{1,0:T(8,128)S(1)}, bf16[192,512]{1,0:T(8,128)(2,1)S(1)}, bf16[192,512]{1,0:T(8,128)(2,1)S(1)}, f32[96,256]{1,0:T(8,128)S(1)}, f32[...) custom-call(f32[2,256,1024]{2,1,0:T(8,128)S(1)} %bitcast.6, ...), custom_call_target="tpu_custom_call" | custom-call | flops 1000000 | bytes 1048576 | tf_op jit(solution)/shard_map/pallas_call | solution.py:591
  15.4 0.0 copy-start.2
  15.4 0.3 collective-permute-done.1.ha
  15.7 0.6 shard_map.79
  16.3 5.4 %collective-permute-done.hb = f32[256,512]{1,0:T(8,128)S(1)} collective-permute-done((f32[256,512]{1,0:T(8,128)S(1)}, f32[256,512]{1,0:T(8,128)S(1)}, u32[]{:S(2)}, u32[]{:S(2)}) %collective-permute-start) | collective-permute-done | bytes 524320 | tf_op jit(solution)/shard_map/ppermute | solution.py:619
  21.8 0.8 %shard_map.80 = (f32[256,512]{1,0:T(8,128)S(1)}, f32[48,256]{1,0:T(8,128)S(1)}, f32[48,256]{1,0:T(8,128)S(1)}) custom-call(f32[256,512]{1,0:T(8,128)S(1)} %get-tuple-element.27.fa, f32[256,512]{1,0:T(8,128)S(1)} %collective-permute-done.hb, f32[256,512]{1,0:T(8,128)S(1)} %get-tuple-element.29.infl, f32[256,128]{1,0:T(8,128)S(1)} %get-tuple-element.30.cols, ...), custom_call_target="tpu_custom_call" | custom-call | flops 1000000 | bytes 1048576 | tf_op jit(solution)/shard_map/pallas_call | solution.py:591
  22.6 0.1 collective-permute-start.2
  22.7 1.2 %collective-permute-done.2 = f32[48,256]{1,0:T(8,128)S(1)} collective-permute-done((f32[48,256]{1,0:T(8,128)S(1)}, f32[48,256]{1,0:T(8,128)S(1)}, u32[]{:S(2)}, u32[]{:S(2)}) %collective-permute-start.2) | collective-permute-done | bytes 49184 | tf_op jit(solution)/shard_map/ppermute | solution.py:643
  23.9 1.7 %collective-permute-start.3 = (f32[48,256]{1,0:T(8,128)S(1)}, f32[48,256]{1,0:T(8,128)S(1)}, u32[]{:S(2)}, u32[]{:S(2)}) collective-permute-start(f32[48,256]{1,0:T(8,128)S(1)} %add.15), channel_id=1, source_target_pairs={{0,2},{2,0},{1,3},{3,1},{4,6},{6,4},{5,7},{7,5},{8,10},{10,8},{9,1... | collective-permute-start | bytes 147464 | tf_op jit(solution)/shard_map/ppermute | solution.py:644
  25.6 2.5 %collective-permute-done.3 = f32[48,256]{1,0:T(8,128)S(1)} collective-permute-done((f32[48,256]{1,0:T(8,128)S(1)}, f32[48,256]{1,0:T(8,128)S(1)}, u32[]{:S(2)}, u32[]{:S(2)}) %collective-permute-start.3) | collective-permute-done | bytes 49184 | tf_op jit(solution)/shard_map/ppermute | solution.py:644
  28.1 2.0 %collective-permute-start.4 = (f32[48,256]{1,0:T(8,128)S(1)}, f32[48,256]{1,0:T(8,128)S(1)}, u32[]{:S(2)}, u32[]{:S(2)}) collective-permute-start(f32[48,256]{1,0:T(8,128)S(1)} %add.16), channel_id=1, source_target_pairs={{0,4},{4,0},{8,12},{12,8},{16,20},{20,16},{24,28},{28,24},{1,5},{5... | collective-permute-start | bytes 147464 | tf_op jit(solution)/shard_map/ppermute | solution.py:650
  30.1 0.0 collective-permute-start.8
  30.1 2.2 %collective-permute-done.4 = f32[48,256]{1,0:T(8,128)S(1)} collective-permute-done((f32[48,256]{1,0:T(8,128)S(1)}, f32[48,256]{1,0:T(8,128)S(1)}, u32[]{:S(2)}, u32[]{:S(2)}) %collective-permute-start.4) | collective-permute-done | bytes 49184 | tf_op jit(solution)/shard_map/ppermute | solution.py:650
  32.3 5.8 %collective-permute-start.10 = (f32[256,512]{1,0:T(8,128)S(1)}, f32[256,512]{1,0:T(8,128)S(1)}, u32[]{:S(2)}, u32[]{:S(2)}) collective-permute-start(f32[256,512]{1,0:T(8,128)S(1)} %get-tuple-element.47.rb), channel_id=1, source_target_pairs={{32,64},{64,32},{96,128},{128,96},{160,192},{192,160},{33,65},{65,... | collective-permute-start | bytes 1572872 | tf_op jit(solution)/shard_map/ppermute | solution.py:619
  38.1 3.4 %collective-permute-start.5 = (f32[48,256]{1,0:T(8,128)S(1)}, f32[48,256]{1,0:T(8,128)S(1)}, u32[]{:S(2)}, u32[]{:S(2)}) collective-permute-start(f32[48,256]{1,0:T(8,128)S(1)} %add.17), channel_id=1, source_target_pairs={{0,8},{8,0},{4,12},{12,4},{16,24},{24,16},{20,28},{28,20},{1,9},{9... | collective-permute-start | bytes 147464 | tf_op jit(solution)/shard_map/ppermute | solution.py:650
  41.4 2.1 %collective-permute-done.5 = f32[48,256]{1,0:T(8,128)S(1)} collective-permute-done((f32[48,256]{1,0:T(8,128)S(1)}, f32[48,256]{1,0:T(8,128)S(1)}, u32[]{:S(2)}, u32[]{:S(2)}) %collective-permute-start.5) | collective-permute-done | bytes 49184 | tf_op jit(solution)/shard_map/ppermute | solution.py:650
  43.5 6.1 %collective-permute-start.6 = (f32[48,256]{1,0:T(8,128)S(1)}, f32[48,256]{1,0:T(8,128)S(1)}, u32[]{:S(2)}, u32[]{:S(2)}) collective-permute-start(f32[48,256]{1,0:T(8,128)S(1)} %add.18), channel_id=1, source_target_pairs={{0,24},{24,0},{4,28},{28,4},{8,16},{16,8},{12,20},{20,12},{1,25},{... | collective-permute-start | bytes 147464 | tf_op jit(solution)/shard_map/ppermute | solution.py:650
  49.6 2.1 %collective-permute-done.6 = f32[48,256]{1,0:T(8,128)S(1)} collective-permute-done((f32[48,256]{1,0:T(8,128)S(1)}, f32[48,256]{1,0:T(8,128)S(1)}, u32[]{:S(2)}, u32[]{:S(2)}) %collective-permute-start.6) | collective-permute-done | bytes 49184 | tf_op jit(solution)/shard_map/ppermute | solution.py:650
  51.7 0.1 collective-permute-start.7
  51.8 1.2 %collective-permute-done.7.other = f32[48,256]{1,0:T(8,128)S(1)} collective-permute-done((f32[48,256]{1,0:T(8,128)S(1)}, f32[48,256]{1,0:T(8,128)S(1)}, u32[]{:S(2)}, u32[]{:S(2)}) %collective-permute-start.7) | collective-permute-done | bytes 49184 | tf_op jit(solution)/shard_map/ppermute | solution.py:652
  53.0 0.0 copy-done.2
  53.0 1.5 %shard_map.81 = (f32[24,256]{1,0:T(8,128)S(1)}, f32[24,256]{1,0:T(8,128)S(1)}, f32[16,256]{1,0:T(8,128)S(1)}, f32[16,256]{1,0:T(8,128)S(1)}) custom-call(f32[48,256]{1,0:T(8,128)S(1)} %add.19.mine, f32[48,256]{1,0:T(8,128)S(1)} %collective-permute-done.7.other, f32[208,256]{1,0:T(8,128)S(1)} %get-tuple-element.39.wall, s32[2,256]{1,0:T(2,128)S(1)} %reshape.22.type_ref, ...), custom_call_target="tpu_custom_call" | custom-call | flops 1000000 | bytes 1048576 | tf_op jit(solution)/shard_map/pallas_call | solution.py:591
  54.5 0.1 collective-permute-start.9
  54.6 3.7 %collective-permute-start.11 = (f32[24,256]{1,0:T(8,128)S(1)}, f32[24,256]{1,0:T(8,128)S(1)}, u32[]{:S(2)}, u32[]{:S(2)}) collective-permute-start(f32[24,256]{1,0:T(8,128)S(1)} %get-tuple-element.48), channel_id=1, source_target_pairs={{32,64},{64,32},{96,128},{128,96},{160,192},{192,160},{33,65},{65,... | collective-permute-start | bytes 73736 | tf_op jit(solution)/shard_map/ppermute | solution.py:619
  58.3 1.4 %shard_map.82 = (f32[256,512]{1,0:T(8,128)S(1)}, f32[256,512]{1,0:T(8,128)S(1)}, f32[256,512]{1,0:T(8,128)S(1)}) custom-call(f32[256,512]{1,0:T(8,128)S(1)} %get-tuple-element.44.ra, f32[256,512]{1,0:T(8,128)S(1)} %get-tuple-element.47.rb, f32[16,256]{1,0:T(8,128)S(1)} %get-tuple-element.40.state, f32[256,512]{1,0:T(8,128)S(1)} %get-tuple-element.41.wall_bulk, ...), custom_call_target="tpu_custom_call" | custom-call | flops 1000000 | bytes 1048576 | tf_op jit(solution)/shard_map/pallas_call | solution.py:591
  59.7 0.0 collective-permute-done.9.from_a
  59.7 0.0 collective-permute-done.8.ha
  59.7 1.0 %shard_map.83.pb = f32[256,512]{1,0:T(8,128)S(1)} custom-call(f32[256,512]{1,0:T(8,128)S(1)} %collective-permute-done.8.ha, f32[24,256]{1,0:T(8,128)S(1)} %collective-permute-done.9.from_a, f32[256,512]{1,0:T(8,128)S(1)} %get-tuple-element.41.wall_bulk), custom_call_target="tpu_custom_call" | custom-call | flops 1000000 | bytes 1048576 | tf_op jit(solution)/shard_map/pallas_call | solution.py:591
  60.7 3.2 %collective-permute-done.11.from_b = f32[24,256]{1,0:T(8,128)S(1)} collective-permute-done((f32[24,256]{1,0:T(8,128)S(1)}, f32[24,256]{1,0:T(8,128)S(1)}, u32[]{:S(2)}, u32[]{:S(2)}) %collective-permute-start.11) | collective-permute-done | bytes 24608 | tf_op jit(solution)/shard_map/ppermute | solution.py:619
  64.0 0.0 collective-permute-done.10.hb
  64.0 3.5 %shard_map.84 = (f32[256,1024]{1,0:T(8,128)}, f32[8,16,16]{2,1,0:T(8,128)}) custom-call(f32[256,512]{1,0:T(8,128)S(1)} %get-tuple-element.42.ca, f32[256,512]{1,0:T(8,128)S(1)} %get-tuple-element.43.cb, f32[256,512]{1,0:T(8,128)S(1)} %shard_map.83.pb, f32[256,512]{1,0:T(8,128)S(1)} %get-tuple-element.46.ghost, f32[256,512]{1,0:T(8,128)S(1)} %collective-permute-done.10.hb, ...), custom_call_target="tpu_custom_call" | custom-call | flops 1000000 | bytes 1048576 | tf_op jit(solution)/shard_map/pallas_call | solution.py:591
  (5 shorter events, 0.0 us)
Async XLA Ops:
  0.6 1.2 %copy-start.1 = (f32[1,16,16,1024]{3,2,1,0:T(8,128)S(1)}, f32[1,16,16,1024]{3,2,1,0:T(8,128)}, u32[]{:S(2)}) copy-start(f32[1,16,16,1024]{3,2,1,0:T(8,128)} %param.6) | copy-start | bytes 3145732
  2.0 13.8 %collective-permute-start.1 = (f32[256,512]{1,0:T(8,128)S(1)}, f32[256,512]{1,0:T(8,128)S(1)}, u32[]{:S(2)}, u32[]{:S(2)}) collective-permute-start(f32[256,512]{1,0:T(8,128)S(1)} %get-tuple-element.27.fa), channel_id=1, source_target_pairs={{0,32},{32,0},{64,96},{96,64},{128,160},{160,128},{192,224},{224,1... | collective-permute-start | bytes 1572872 | tf_op jit(solution)/shard_map/ppermute | solution.py:620
  2.9 18.9 %collective-permute-start = (f32[256,512]{1,0:T(8,128)S(1)}, f32[256,512]{1,0:T(8,128)S(1)}, u32[]{:S(2)}, u32[]{:S(2)}) collective-permute-start(f32[256,512]{1,0:T(8,128)S(1)} %get-tuple-element.28.fb), channel_id=1, source_target_pairs={{32,64},{64,32},{96,128},{128,96},{160,192},{192,160},{33,65},{65,... | collective-permute-start | bytes 1572872 | tf_op jit(solution)/shard_map/ppermute | solution.py:619
  10.2 1.6 %copy-start = (f32[2,16,16,1024]{3,2,1,0:T(8,128)S(1)}, f32[2,16,16,1024]{3,2,1,0:T(8,128)}, u32[]{:S(2)}) copy-start(f32[2,16,16,1024]{3,2,1,0:T(8,128)} %param.7) | copy-start | bytes 6291460
  11.8 0.9 %copy-start.3 = (f32[2,192,96]{2,1,0:T(8,128)S(1)}, f32[2,192,96]{2,1,0:T(8,128)}, u32[]{:S(2)}) copy-start(f32[2,192,96]{2,1,0:T(8,128)} %constant.5.clone.tables) | copy-start | bytes 442372
  15.4 37.6 %copy-start.2 = (bf16[256,96]{1,0:T(8,128)(2,1)S(1)}, bf16[256,96]{1,0:T(8,128)(2,1)}, u32[]{:S(2)}) copy-start(bf16[256,96]{1,0:T(8,128)(2,1)} %constant.4.clone.table) | copy-start | bytes 147460
  22.6 1.3 %collective-permute-start.2 = (f32[48,256]{1,0:T(8,128)S(1)}, f32[48,256]{1,0:T(8,128)S(1)}, u32[]{:S(2)}, u32[]{:S(2)}) collective-permute-start(f32[48,256]{1,0:T(8,128)S(1)} %get-tuple-element.38), channel_id=1, source_target_pairs={{0,1},{1,0},{2,3},{3,2},{4,5},{5,4},{6,7},{7,6},{8,9},{9,8},{10,11... | collective-permute-start | bytes 147464 | tf_op jit(solution)/shard_map/ppermute | solution.py:643
  23.9 4.2 %collective-permute-start.3 = (f32[48,256]{1,0:T(8,128)S(1)}, f32[48,256]{1,0:T(8,128)S(1)}, u32[]{:S(2)}, u32[]{:S(2)}) collective-permute-start(f32[48,256]{1,0:T(8,128)S(1)} %add.15), channel_id=1, source_target_pairs={{0,2},{2,0},{1,3},{3,1},{4,6},{6,4},{5,7},{7,5},{8,10},{10,8},{9,1... | collective-permute-start | bytes 147464 | tf_op jit(solution)/shard_map/ppermute | solution.py:644
  28.1 4.2 %collective-permute-start.4 = (f32[48,256]{1,0:T(8,128)S(1)}, f32[48,256]{1,0:T(8,128)S(1)}, u32[]{:S(2)}, u32[]{:S(2)}) collective-permute-start(f32[48,256]{1,0:T(8,128)S(1)} %add.16), channel_id=1, source_target_pairs={{0,4},{4,0},{8,12},{12,8},{16,20},{20,16},{24,28},{28,24},{1,5},{5... | collective-permute-start | bytes 147464 | tf_op jit(solution)/shard_map/ppermute | solution.py:650
  30.1 29.6 %collective-permute-start.8 = (f32[256,512]{1,0:T(8,128)S(1)}, f32[256,512]{1,0:T(8,128)S(1)}, u32[]{:S(2)}, u32[]{:S(2)}) collective-permute-start(f32[256,512]{1,0:T(8,128)S(1)} %get-tuple-element.44.ra), channel_id=1, source_target_pairs={{0,32},{32,0},{64,96},{96,64},{128,160},{160,128},{192,224},{224,1... | collective-permute-start | bytes 1572872 | tf_op jit(solution)/shard_map/ppermute | solution.py:620
  32.3 31.7 %collective-permute-start.10 = (f32[256,512]{1,0:T(8,128)S(1)}, f32[256,512]{1,0:T(8,128)S(1)}, u32[]{:S(2)}, u32[]{:S(2)}) collective-permute-start(f32[256,512]{1,0:T(8,128)S(1)} %get-tuple-element.47.rb), channel_id=1, source_target_pairs={{32,64},{64,32},{96,128},{128,96},{160,192},{192,160},{33,65},{65,... | collective-permute-start | bytes 1572872 | tf_op jit(solution)/shard_map/ppermute | solution.py:619
  38.1 5.4 %collective-permute-start.5 = (f32[48,256]{1,0:T(8,128)S(1)}, f32[48,256]{1,0:T(8,128)S(1)}, u32[]{:S(2)}, u32[]{:S(2)}) collective-permute-start(f32[48,256]{1,0:T(8,128)S(1)} %add.17), channel_id=1, source_target_pairs={{0,8},{8,0},{4,12},{12,4},{16,24},{24,16},{20,28},{28,20},{1,9},{9... | collective-permute-start | bytes 147464 | tf_op jit(solution)/shard_map/ppermute | solution.py:650
  43.5 8.2 %collective-permute-start.6 = (f32[48,256]{1,0:T(8,128)S(1)}, f32[48,256]{1,0:T(8,128)S(1)}, u32[]{:S(2)}, u32[]{:S(2)}) collective-permute-start(f32[48,256]{1,0:T(8,128)S(1)} %add.18), channel_id=1, source_target_pairs={{0,24},{24,0},{4,28},{28,4},{8,16},{16,8},{12,20},{20,12},{1,25},{... | collective-permute-start | bytes 147464 | tf_op jit(solution)/shard_map/ppermute | solution.py:650
  51.7 1.3 %collective-permute-start.7 = (f32[48,256]{1,0:T(8,128)S(1)}, f32[48,256]{1,0:T(8,128)S(1)}, u32[]{:S(2)}, u32[]{:S(2)}) collective-permute-start(f32[48,256]{1,0:T(8,128)S(1)} %add.19.mine), channel_id=1, source_target_pairs={{0,1},{1,0},{2,3},{3,2},{4,5},{5,4},{6,7},{7,6},{8,9},{9,8},{10,11... | collective-permute-start | bytes 147464 | tf_op jit(solution)/shard_map/ppermute | solution.py:652
  54.5 5.2 %collective-permute-start.9 = (f32[24,256]{1,0:T(8,128)S(1)}, f32[24,256]{1,0:T(8,128)S(1)}, u32[]{:S(2)}, u32[]{:S(2)}) collective-permute-start(f32[24,256]{1,0:T(8,128)S(1)} %get-tuple-element.45), channel_id=1, source_target_pairs={{0,32},{32,0},{64,96},{96,64},{128,160},{160,128},{192,224},{224,1... | collective-permute-start | bytes 73736 | tf_op jit(solution)/shard_map/ppermute | solution.py:620
  54.6 9.3 %collective-permute-start.11 = (f32[24,256]{1,0:T(8,128)S(1)}, f32[24,256]{1,0:T(8,128)S(1)}, u32[]{:S(2)}, u32[]{:S(2)}) collective-permute-start(f32[24,256]{1,0:T(8,128)S(1)} %get-tuple-element.48), channel_id=1, source_target_pairs={{32,64},{64,32},{96,128},{128,96},{160,192},{192,160},{33,65},{65,... | collective-permute-start | bytes 73736 | tf_op jit(solution)/shard_map/ppermute | solution.py:619

commit v4 on v3

--- a/solution.py
+++ b/solution.py
@@ -296,7 +296,7 @@
         wall_bulk[at, :] = c[:, 3:4] * jnp.exp(speed_sq * c[:, 2:3])
         return carry
 
-    lax.fori_loop(0, 16, step, 0, unroll=4)
+    lax.fori_loop(0, 16, step, 0, unroll=8)
     for w, parts in ((wa, pa), (wb, pb)):
         high, low = split(w[...])
         parts[:ROWS, :] = high
@@ -335,7 +335,7 @@
         rb[at, :] = transport_block(fb[at, :], fb[upwind_y(p, i), :], ha[at, :], weights)
         return carry
 
-    lax.fori_loop(0, 16, step, 0, unroll=4)
+    lax.fori_loop(0, 16, step, 0, unroll=8)
     rows[...] = pre[...] + dot_parts(wb[...], rb[...], 1)
 
 
@@ -352,7 +352,7 @@
         ra[at, :] = transport_block(value, fa[upwind_y(p, i), :], plane, weights)
         return carry
 
-    lax.fori_loop(0, 16, step, 0, unroll=4)
+    lax.fori_loop(0, 16, step, 0, unroll=8)
     rows = rows_b[...] + dot_parts(wa[...], ra[...], 1)
     north = p % 2 == 1
     top, bottom = rows[:HROWS], rows[HROWS:]
@@ -498,7 +498,7 @@
         ghost[at, :] = infl[at, :] * face[:, 0:1] + k[14] * w + face[:, 1:2] * value
         return carry
 
-    lax.fori_loop(0, 16, step, 0, unroll=4)
+    lax.fori_loop(0, 16, step, 0, unroll=8)
 
 
 def halo_kernel(ha, from_a, wall_bulk, pb, work):
@@ -522,7 +522,7 @@
         pb[at, :] = relaxed(ha[at, :] + k[13] * wall_bulk[at, :], k, shared_part(k, cy, cz), 1)
         return carry
 
-    lax.fori_loop(0, 16, step, 0, unroll=4)
+    lax.fori_loop(0, 16, step, 0, unroll=8)
 
 
 def final_kernel(

time: 67.9 us -> 68 us (level)
  transfers between devices with their start and end apart: 12 -> 12, of which waited for: 9 -> 9; matrix products, arithmetic and copies ran while one was open for 2% -> 2% of each run, Pallas kernels for 11% -> 10%
where the time goes in v4:
time: 68 us; the launch traced here: 67.6 us
  starting transfers between devices  29.6 us (44%)
  waiting for transfers between devices  20.5 us (30%)
  Pallas kernels  11.2 us (16%)
  local copies, waits for them, and re-layouts  5.34 us (8%)
  between operations  0.94 us (1%)
    ppermute x3, starting transfers between devices, swap_planes(): b = lax.ppermute(b, 'space', PAIRS_B)  15.3 us
    ppermute x3, starting transfers between devices, body(): part = part + lax.ppermute(part, 'z', pairs)  11.5 us
    pallas_call x8, Pallas kernels, call(): pl.pallas_call(kernel, out_shape=[jax.ShapeDtypeStruct(s, jnp.bfloat16 if...  11.2 us
    ppermute x3, waiting for transfers between devices, swap_planes(): b = lax.ppermute(b, 'space', PAIRS_B)  8.74 us
    ppermute x3, waiting for transfers between devices, body(): part = part + lax.ppermute(part, 'z', pairs)  6.32 us
    unnamed x8, local copies, waits for them, and re-layouts  3.74 us
    ppermute x1, waiting for transfers between devices, body(): part = part + lax.ppermute(part, 'ylo', SWAP)  2.51 us
    ppermute x1, starting transfers between devices, body(): part = part + lax.ppermute(part, 'ylo', SWAP)  1.66 us
  transfers between devices with their start and end apart: 12, of which 9 were waited for; matrix products, arithmetic and copies ran while one was open for 2% of the time, Pallas kernels for 10%

profile of v4, /device:TPU:6, one launch (start us, length us, event | category | flops | bytes accessed | tf_op | source)
XLA Modules:
  0.0 67.6 jit_solution(16906663934491026162)
XLA Ops:
  0.6 0.0 copy-start.1
  0.6 1.2 %copy-done.1 = f32[1,16,16,1024]{3,2,1,0:T(8,128)S(1)} copy-done((f32[1,16,16,1024]{3,2,1,0:T(8,128)S(1)}, f32[1,16,16,1024]{3,2,1,0:T(8,128)}, u32[]{:S(2)}) %copy-start.1) | copy-done | bytes 1048600
  1.9 0.1 shard_map.77
  2.0 0.9 %collective-permute-start.1 = (f32[256,512]{1,0:T(8,128)S(1)}, f32[256,512]{1,0:T(8,128)S(1)}, u32[]{:S(2)}, u32[]{:S(2)}) collective-permute-start(f32[256,512]{1,0:T(8,128)S(1)} %get-tuple-element.27.fa), channel_id=1, source_target_pairs={{0,32},{32,0},{64,96},{96,64},{128,160},{160,128},{192,224},{224,1... | collective-permute-start | bytes 1572872 | tf_op jit(solution)/shard_map/ppermute | solution.py:620
  2.9 5.7 %collective-permute-start = (f32[256,512]{1,0:T(8,128)S(1)}, f32[256,512]{1,0:T(8,128)S(1)}, u32[]{:S(2)}, u32[]{:S(2)}) collective-permute-start(f32[256,512]{1,0:T(8,128)S(1)} %get-tuple-element.28.fb), channel_id=1, source_target_pairs={{32,64},{64,32},{96,128},{128,96},{160,192},{192,160},{33,65},{65,... | collective-permute-start | bytes 1572872 | tf_op jit(solution)/shard_map/ppermute | solution.py:619
  8.6 0.8 %reshape.21.temp_ref = f32[2,256]{1,0:T(2,128)S(1)} reshape(f32[2,16,16]{2,1,0:T(8,128)} %param.8) | data formatting | bytes 4096 | tf_op jit(solution)/shard_map/reshape | solution.py:628
  9.4 0.8 %reshape.22.type_ref = s32[2,256]{1,0:T(2,128)S(1)} reshape(s32[2,16,16]{2,1,0:T(8,128)} %param.9) | data formatting | bytes 4096 | tf_op jit(solution)/shard_map/reshape | solution.py:629
  10.2 0.0 copy-start
  10.2 1.6 %copy-done = f32[2,16,16,1024]{3,2,1,0:T(8,128)S(1)} copy-done((f32[2,16,16,1024]{3,2,1,0:T(8,128)S(1)}, f32[2,16,16,1024]{3,2,1,0:T(8,128)}, u32[]{:S(2)}) %copy-start) | copy-done | bytes 2097176
  11.8 0.0 copy-start.3
  11.8 0.9 %copy-done.3 = f32[2,192,96]{2,1,0:T(8,128)S(1)} copy-done((f32[2,192,96]{2,1,0:T(8,128)S(1)}, f32[2,192,96]{2,1,0:T(8,128)}, u32[]{:S(2)}) %copy-start.3) | copy-done | bytes 147480
  12.7 2.6 %shard_map.78 = (f32[256,512]{1,0:T(8,128)S(1)}, bf16[192,512]{1,0:T(8,128)(2,1)S(1)}, bf16[192,512]{1,0:T(8,128)(2,1)S(1)}, f32[96,256]{1,0:T(8,128)S(1)}, f32[...) custom-call(f32[2,256,1024]{2,1,0:T(8,128)S(1)} %bitcast.6, ...), custom_call_target="tpu_custom_call" | custom-call | flops 1000000 | bytes 1048576 | tf_op jit(solution)/shard_map/pallas_call | solution.py:591
  15.3 0.0 copy-start.2
  15.3 0.5 collective-permute-done.1.ha
  15.7 0.6 shard_map.79
  16.3 5.4 %collective-permute-done.hb = f32[256,512]{1,0:T(8,128)S(1)} collective-permute-done((f32[256,512]{1,0:T(8,128)S(1)}, f32[256,512]{1,0:T(8,128)S(1)}, u32[]{:S(2)}, u32[]{:S(2)}) %collective-permute-start) | collective-permute-done | bytes 524320 | tf_op jit(solution)/shard_map/ppermute | solution.py:619
  21.8 0.7 %shard_map.80 = (f32[256,512]{1,0:T(8,128)S(1)}, f32[48,256]{1,0:T(8,128)S(1)}, f32[48,256]{1,0:T(8,128)S(1)}) custom-call(f32[256,512]{1,0:T(8,128)S(1)} %get-tuple-element.27.fa, f32[256,512]{1,0:T(8,128)S(1)} %collective-permute-done.hb, f32[256,512]{1,0:T(8,128)S(1)} %get-tuple-element.29.infl, f32[256,128]{1,0:T(8,128)S(1)} %get-tuple-element.30.cols, ...), custom_call_target="tpu_custom_call" | custom-call | flops 1000000 | bytes 1048576 | tf_op jit(solution)/shard_map/pallas_call | solution.py:591
  22.5 0.1 collective-permute-start.2
  22.6 1.2 %collective-permute-done.2 = f32[48,256]{1,0:T(8,128)S(1)} collective-permute-done((f32[48,256]{1,0:T(8,128)S(1)}, f32[48,256]{1,0:T(8,128)S(1)}, u32[]{:S(2)}, u32[]{:S(2)}) %collective-permute-start.2) | collective-permute-done | bytes 49184 | tf_op jit(solution)/shard_map/ppermute | solution.py:643
  23.8 1.7 %collective-permute-start.3 = (f32[48,256]{1,0:T(8,128)S(1)}, f32[48,256]{1,0:T(8,128)S(1)}, u32[]{:S(2)}, u32[]{:S(2)}) collective-permute-start(f32[48,256]{1,0:T(8,128)S(1)} %add.15), channel_id=1, source_target_pairs={{0,2},{2,0},{1,3},{3,1},{4,6},{6,4},{5,7},{7,5},{8,10},{10,8},{9,1... | collective-permute-start | bytes 147464 | tf_op jit(solution)/shard_map/ppermute | solution.py:644
  25.5 2.5 %collective-permute-done.3 = f32[48,256]{1,0:T(8,128)S(1)} collective-permute-done((f32[48,256]{1,0:T(8,128)S(1)}, f32[48,256]{1,0:T(8,128)S(1)}, u32[]{:S(2)}, u32[]{:S(2)}) %collective-permute-start.3) | collective-permute-done | bytes 49184 | tf_op jit(solution)/shard_map/ppermute | solution.py:644
  28.0 2.0 %collective-permute-start.4 = (f32[48,256]{1,0:T(8,128)S(1)}, f32[48,256]{1,0:T(8,128)S(1)}, u32[]{:S(2)}, u32[]{:S(2)}) collective-permute-start(f32[48,256]{1,0:T(8,128)S(1)} %add.16), channel_id=1, source_target_pairs={{0,4},{4,0},{8,12},{12,8},{16,20},{20,16},{24,28},{28,24},{1,5},{5... | collective-permute-start | bytes 147464 | tf_op jit(solution)/shard_map/ppermute | solution.py:650
  30.0 0.0 collective-permute-start.8
  30.0 2.2 %collective-permute-done.4 = f32[48,256]{1,0:T(8,128)S(1)} collective-permute-done((f32[48,256]{1,0:T(8,128)S(1)}, f32[48,256]{1,0:T(8,128)S(1)}, u32[]{:S(2)}, u32[]{:S(2)}) %collective-permute-start.4) | collective-permute-done | bytes 49184 | tf_op jit(solution)/shard_map/ppermute | solution.py:650
  32.2 5.8 %collective-permute-start.10 = (f32[256,512]{1,0:T(8,128)S(1)}, f32[256,512]{1,0:T(8,128)S(1)}, u32[]{:S(2)}, u32[]{:S(2)}) collective-permute-start(f32[256,512]{1,0:T(8,128)S(1)} %get-tuple-element.47.rb), channel_id=1, source_target_pairs={{32,64},{64,32},{96,128},{128,96},{160,192},{192,160},{33,65},{65,... | collective-permute-start | bytes 1572872 | tf_op jit(solution)/shard_map/ppermute | solution.py:619
  38.0 3.4 %collective-permute-start.5 = (f32[48,256]{1,0:T(8,128)S(1)}, f32[48,256]{1,0:T(8,128)S(1)}, u32[]{:S(2)}, u32[]{:S(2)}) collective-permute-start(f32[48,256]{1,0:T(8,128)S(1)} %add.17), channel_id=1, source_target_pairs={{0,8},{8,0},{4,12},{12,4},{16,24},{24,16},{20,28},{28,20},{1,9},{9... | collective-permute-start | bytes 147464 | tf_op jit(solution)/shard_map/ppermute | solution.py:650
  41.4 2.1 %collective-permute-done.5 = f32[48,256]{1,0:T(8,128)S(1)} collective-permute-done((f32[48,256]{1,0:T(8,128)S(1)}, f32[48,256]{1,0:T(8,128)S(1)}, u32[]{:S(2)}, u32[]{:S(2)}) %collective-permute-start.5) | collective-permute-done | bytes 49184 | tf_op jit(solution)/shard_map/ppermute | solution.py:650
  43.4 6.1 %collective-permute-start.6 = (f32[48,256]{1,0:T(8,128)S(1)}, f32[48,256]{1,0:T(8,128)S(1)}, u32[]{:S(2)}, u32[]{:S(2)}) collective-permute-start(f32[48,256]{1,0:T(8,128)S(1)} %add.18), channel_id=1, source_target_pairs={{0,24},{24,0},{4,28},{28,4},{8,16},{16,8},{12,20},{20,12},{1,25},{... | collective-permute-start | bytes 147464 | tf_op jit(solution)/shard_map/ppermute | solution.py:650
  49.6 2.1 %collective-permute-done.6 = f32[48,256]{1,0:T(8,128)S(1)} collective-permute-done((f32[48,256]{1,0:T(8,128)S(1)}, f32[48,256]{1,0:T(8,128)S(1)}, u32[]{:S(2)}, u32[]{:S(2)}) %collective-permute-start.6) | collective-permute-done | bytes 49184 | tf_op jit(solution)/shard_map/ppermute | solution.py:650
  51.6 0.1 collective-permute-start.7
  51.7 1.2 %collective-permute-done.7.other = f32[48,256]{1,0:T(8,128)S(1)} collective-permute-done((f32[48,256]{1,0:T(8,128)S(1)}, f32[48,256]{1,0:T(8,128)S(1)}, u32[]{:S(2)}, u32[]{:S(2)}) %collective-permute-start.7) | collective-permute-done | bytes 49184 | tf_op jit(solution)/shard_map/ppermute | solution.py:652
  53.0 0.0 copy-done.2
  53.0 1.5 %shard_map.81 = (f32[24,256]{1,0:T(8,128)S(1)}, f32[24,256]{1,0:T(8,128)S(1)}, f32[16,256]{1,0:T(8,128)S(1)}, f32[16,256]{1,0:T(8,128)S(1)}) custom-call(f32[48,256]{1,0:T(8,128)S(1)} %add.19.mine, f32[48,256]{1,0:T(8,128)S(1)} %collective-permute-done.7.other, f32[208,256]{1,0:T(8,128)S(1)} %get-tuple-element.39.wall, s32[2,256]{1,0:T(2,128)S(1)} %reshape.22.type_ref, ...), custom_call_target="tpu_custom_call" | custom-call | flops 1000000 | bytes 1048576 | tf_op jit(solution)/shard_map/pallas_call | solution.py:591
  54.5 0.1 collective-permute-start.9
  54.6 3.9 %collective-permute-start.11 = (f32[24,256]{1,0:T(8,128)S(1)}, f32[24,256]{1,0:T(8,128)S(1)}, u32[]{:S(2)}, u32[]{:S(2)}) collective-permute-start(f32[24,256]{1,0:T(8,128)S(1)} %get-tuple-element.48), channel_id=1, source_target_pairs={{32,64},{64,32},{96,128},{128,96},{160,192},{192,160},{33,65},{65,... | collective-permute-start | bytes 73736 | tf_op jit(solution)/shard_map/ppermute | solution.py:619
  58.4 1.2 %shard_map.82 = (f32[256,512]{1,0:T(8,128)S(1)}, f32[256,512]{1,0:T(8,128)S(1)}, f32[256,512]{1,0:T(8,128)S(1)}) custom-call(f32[256,512]{1,0:T(8,128)S(1)} %get-tuple-element.44.ra, f32[256,512]{1,0:T(8,128)S(1)} %get-tuple-element.47.rb, f32[16,256]{1,0:T(8,128)S(1)} %get-tuple-element.40.state, f32[256,512]{1,0:T(8,128)S(1)} %get-tuple-element.41.wall_bulk, ...), custom_call_target="tpu_custom_call" | custom-call | flops 1000000 | bytes 1048576 | tf_op jit(solution)/shard_map/pallas_call | solution.py:591
  59.7 0.0 collective-permute-done.9.from_a
  59.7 0.0 collective-permute-done.8.ha
  59.7 0.9 %shard_map.83.pb = f32[256,512]{1,0:T(8,128)S(1)} custom-call(f32[256,512]{1,0:T(8,128)S(1)} %collective-permute-done.8.ha, f32[24,256]{1,0:T(8,128)S(1)} %collective-permute-done.9.from_a, f32[256,512]{1,0:T(8,128)S(1)} %get-tuple-element.41.wall_bulk), custom_call_target="tpu_custom_call" | custom-call | flops 1000000 | bytes 1048576 | tf_op jit(solution)/shard_map/pallas_call | solution.py:591
  60.6 3.3 %collective-permute-done.11.from_b = f32[24,256]{1,0:T(8,128)S(1)} collective-permute-done((f32[24,256]{1,0:T(8,128)S(1)}, f32[24,256]{1,0:T(8,128)S(1)}, u32[]{:S(2)}, u32[]{:S(2)}) %collective-permute-start.11) | collective-permute-done | bytes 24608 | tf_op jit(solution)/shard_map/ppermute | solution.py:619
  63.9 0.0 collective-permute-done.10.hb
  63.9 3.5 %shard_map.84 = (f32[256,1024]{1,0:T(8,128)}, f32[8,16,16]{2,1,0:T(8,128)}) custom-call(f32[256,512]{1,0:T(8,128)S(1)} %get-tuple-element.42.ca, f32[256,512]{1,0:T(8,128)S(1)} %get-tuple-element.43.cb, f32[256,512]{1,0:T(8,128)S(1)} %shard_map.83.pb, f32[256,512]{1,0:T(8,128)S(1)} %get-tuple-element.46.ghost, f32[256,512]{1,0:T(8,128)S(1)} %collective-permute-done.10.hb, ...), custom_call_target="tpu_custom_call" | custom-call | flops 1000000 | bytes 1048576 | tf_op jit(solution)/shard_map/pallas_call | solution.py:591
  (5 shorter events, 0.0 us)
Async XLA Ops:
  0.6 1.2 %copy-start.1 = (f32[1,16,16,1024]{3,2,1,0:T(8,128)S(1)}, f32[1,16,16,1024]{3,2,1,0:T(8,128)}, u32[]{:S(2)}) copy-start(f32[1,16,16,1024]{3,2,1,0:T(8,128)} %param.6) | copy-start | bytes 3145732
  2.0 13.8 %collective-permute-start.1 = (f32[256,512]{1,0:T(8,128)S(1)}, f32[256,512]{1,0:T(8,128)S(1)}, u32[]{:S(2)}, u32[]{:S(2)}) collective-permute-start(f32[256,512]{1,0:T(8,128)S(1)} %get-tuple-element.27.fa), channel_id=1, source_target_pairs={{0,32},{32,0},{64,96},{96,64},{128,160},{160,128},{192,224},{224,1... | collective-permute-start | bytes 1572872 | tf_op jit(solution)/shard_map/ppermute | solution.py:620
  2.9 18.9 %collective-permute-start = (f32[256,512]{1,0:T(8,128)S(1)}, f32[256,512]{1,0:T(8,128)S(1)}, u32[]{:S(2)}, u32[]{:S(2)}) collective-permute-start(f32[256,512]{1,0:T(8,128)S(1)} %get-tuple-element.28.fb), channel_id=1, source_target_pairs={{32,64},{64,32},{96,128},{128,96},{160,192},{192,160},{33,65},{65,... | collective-permute-start | bytes 1572872 | tf_op jit(solution)/shard_map/ppermute | solution.py:619
  10.2 1.6 %copy-start = (f32[2,16,16,1024]{3,2,1,0:T(8,128)S(1)}, f32[2,16,16,1024]{3,2,1,0:T(8,128)}, u32[]{:S(2)}) copy-start(f32[2,16,16,1024]{3,2,1,0:T(8,128)} %param.7) | copy-start | bytes 6291460
  11.8 0.9 %copy-start.3 = (f32[2,192,96]{2,1,0:T(8,128)S(1)}, f32[2,192,96]{2,1,0:T(8,128)}, u32[]{:S(2)}) copy-start(f32[2,192,96]{2,1,0:T(8,128)} %constant.5.clone.tables) | copy-start | bytes 442372
  15.3 37.7 %copy-start.2 = (bf16[256,96]{1,0:T(8,128)(2,1)S(1)}, bf16[256,96]{1,0:T(8,128)(2,1)}, u32[]{:S(2)}) copy-start(bf16[256,96]{1,0:T(8,128)(2,1)} %constant.4.clone.table) | copy-start | bytes 147460
  22.5 1.3 %collective-permute-start.2 = (f32[48,256]{1,0:T(8,128)S(1)}, f32[48,256]{1,0:T(8,128)S(1)}, u32[]{:S(2)}, u32[]{:S(2)}) collective-permute-start(f32[48,256]{1,0:T(8,128)S(1)} %get-tuple-element.38), channel_id=1, source_target_pairs={{0,1},{1,0},{2,3},{3,2},{4,5},{5,4},{6,7},{7,6},{8,9},{9,8},{10,11... | collective-permute-start | bytes 147464 | tf_op jit(solution)/shard_map/ppermute | solution.py:643
  23.8 4.2 %collective-permute-start.3 = (f32[48,256]{1,0:T(8,128)S(1)}, f32[48,256]{1,0:T(8,128)S(1)}, u32[]{:S(2)}, u32[]{:S(2)}) collective-permute-start(f32[48,256]{1,0:T(8,128)S(1)} %add.15), channel_id=1, source_target_pairs={{0,2},{2,0},{1,3},{3,1},{4,6},{6,4},{5,7},{7,5},{8,10},{10,8},{9,1... | collective-permute-start | bytes 147464 | tf_op jit(solution)/shard_map/ppermute | solution.py:644
  28.0 4.2 %collective-permute-start.4 = (f32[48,256]{1,0:T(8,128)S(1)}, f32[48,256]{1,0:T(8,128)S(1)}, u32[]{:S(2)}, u32[]{:S(2)}) collective-permute-start(f32[48,256]{1,0:T(8,128)S(1)} %add.16), channel_id=1, source_target_pairs={{0,4},{4,0},{8,12},{12,8},{16,20},{20,16},{24,28},{28,24},{1,5},{5... | collective-permute-start | bytes 147464 | tf_op jit(solution)/shard_map/ppermute | solution.py:650
  30.0 29.7 %collective-permute-start.8 = (f32[256,512]{1,0:T(8,128)S(1)}, f32[256,512]{1,0:T(8,128)S(1)}, u32[]{:S(2)}, u32[]{:S(2)}) collective-permute-start(f32[256,512]{1,0:T(8,128)S(1)} %get-tuple-element.44.ra), channel_id=1, source_target_pairs={{0,32},{32,0},{64,96},{96,64},{128,160},{160,128},{192,224},{224,1... | collective-permute-start | bytes 1572872 | tf_op jit(solution)/shard_map/ppermute | solution.py:620
  32.2 31.7 %collective-permute-start.10 = (f32[256,512]{1,0:T(8,128)S(1)}, f32[256,512]{1,0:T(8,128)S(1)}, u32[]{:S(2)}, u32[]{:S(2)}) collective-permute-start(f32[256,512]{1,0:T(8,128)S(1)} %get-tuple-element.47.rb), channel_id=1, source_target_pairs={{32,64},{64,32},{96,128},{128,96},{160,192},{192,160},{33,65},{65,... | collective-permute-start | bytes 1572872 | tf_op jit(solution)/shard_map/ppermute | solution.py:619
  38.0 5.4 %collective-permute-start.5 = (f32[48,256]{1,0:T(8,128)S(1)}, f32[48,256]{1,0:T(8,128)S(1)}, u32[]{:S(2)}, u32[]{:S(2)}) collective-permute-start(f32[48,256]{1,0:T(8,128)S(1)} %add.17), channel_id=1, source_target_pairs={{0,8},{8,0},{4,12},{12,4},{16,24},{24,16},{20,28},{28,20},{1,9},{9... | collective-permute-start | bytes 147464 | tf_op jit(solution)/shard_map/ppermute | solution.py:650
  43.4 8.2 %collective-permute-start.6 = (f32[48,256]{1,0:T(8,128)S(1)}, f32[48,256]{1,0:T(8,128)S(1)}, u32[]{:S(2)}, u32[]{:S(2)}) collective-permute-start(f32[48,256]{1,0:T(8,128)S(1)} %add.18), channel_id=1, source_target_pairs={{0,24},{24,0},{4,28},{28,4},{8,16},{16,8},{12,20},{20,12},{1,25},{... | collective-permute-start | bytes 147464 | tf_op jit(solution)/shard_map/ppermute | solution.py:650
  51.6 1.3 %collective-permute-start.7 = (f32[48,256]{1,0:T(8,128)S(1)}, f32[48,256]{1,0:T(8,128)S(1)}, u32[]{:S(2)}, u32[]{:S(2)}) collective-permute-start(f32[48,256]{1,0:T(8,128)S(1)} %add.19.mine), channel_id=1, source_target_pairs={{0,1},{1,0},{2,3},{3,2},{4,5},{5,4},{6,7},{7,6},{8,9},{9,8},{10,11... | collective-permute-start | bytes 147464 | tf_op jit(solution)/shard_map/ppermute | solution.py:652
  54.5 5.2 %collective-permute-start.9 = (f32[24,256]{1,0:T(8,128)S(1)}, f32[24,256]{1,0:T(8,128)S(1)}, u32[]{:S(2)}, u32[]{:S(2)}) collective-permute-start(f32[24,256]{1,0:T(8,128)S(1)} %get-tuple-element.45), channel_id=1, source_target_pairs={{0,32},{32,0},{64,96},{96,64},{128,160},{160,128},{192,224},{224,1... | collective-permute-start | bytes 73736 | tf_op jit(solution)/shard_map/ppermute | solution.py:620
  54.6 9.3 %collective-permute-start.11 = (f32[24,256]{1,0:T(8,128)S(1)}, f32[24,256]{1,0:T(8,128)S(1)}, u32[]{:S(2)}, u32[]{:S(2)}) collective-permute-start(f32[24,256]{1,0:T(8,128)S(1)} %get-tuple-element.48), channel_id=1, source_target_pairs={{32,64},{64,32},{96,128},{128,96},{160,192},{192,160},{33,65},{65,... | collective-permute-start | bytes 73736 | tf_op jit(solution)/shard_map/ppermute | solution.py:619
